TPU v7x, 128 devices: a whole 4x4x4 slice. The times are simulated.
128 devices in a mesh: vp: 4 (over x), dp: 32 (over z, y, core).
Axes of the slice: x: 4, y: 4, z: 4, core: 2. Of those that a mesh axis runs over, the one named last changes fastest.
Arguments:
- hidden: bfloat16 [192, 512, 1024], P('dp')
- mask_pos: int32 [192, 77], P('dp')
- labels: int32 [192, 77], P('dp')
- w_trans: bfloat16 [1024, 1024], replicated
- b_trans: float32 [1024], replicated
- ln_gain: float32 [1024], replicated
- ln_bias: float32 [1024], replicated
- emb_table: bfloat16 [30592, 1024], P('vp')
- b_vocab: float32 [30592], P('vp')
Outputs:
- output 1: float32 [], replicated
- output 2: bfloat16 [192, 512, 1024], P('dp')
- output 3: float32 [1024, 1024], replicated
- output 4: float32 [1024], replicated
- output 5: float32 [1024], replicated
- output 6: float32 [1024], replicated
- output 7: float32 [30592, 1024], P('vp')
- output 8: float32 [30592], P('vp')
All inputs are finite; a program needn't handle non-finite values.
Results may differ from a plain program's by a relative error of at most 0.0107114.
Values sent between devices are 32-bit elements.
A program may use at most 1 GiB of HBM per device.

v0:
```python
import jax
import jax.numpy as jnp
from jax import lax
from jax.sharding import PartitionSpec as P

LN_EPS = 1e-5


def head_norm(pre_act, ln_gain, ln_bias):
    gelu_out = jax.nn.gelu(pre_act, approximate=False)
    row_mean = jnp.mean(gelu_out, axis=-1, keepdims=True)
    centered = gelu_out - row_mean
    row_var = jnp.mean(centered * centered, axis=-1, keepdims=True)
    return centered * lax.rsqrt(row_var + LN_EPS) * ln_gain + ln_bias


def solution(mesh):
    n_groups = mesh.shape["dp"]

    def local_step(hidden, mask_pos, labels, w_trans, b_trans, ln_gain, ln_bias, emb_table, b_vocab):
        n_rows, seq_len = hidden.shape[0], hidden.shape[1]
        n_masks = mask_pos.shape[1]
        shard_rows = emb_table.shape[0]
        n_tokens = n_rows * n_masks * n_groups
        row_start = lax.axis_index("vp") * shard_rows
        pos_onehot = (mask_pos[:, :, None] == jnp.arange(seq_len)[None, None, :]).astype(jnp.bfloat16)
        masked_h = jnp.einsum("clt,cte->cle", pos_onehot, hidden, preferred_element_type=jnp.float32).astype(jnp.bfloat16)
        pre_act = jnp.einsum("cle,ef->clf", masked_h, w_trans, preferred_element_type=jnp.float32) + b_trans
        u_norm, head_vjp = jax.vjp(head_norm, pre_act, ln_gain, ln_bias)
        u_bf16 = u_norm.astype(jnp.bfloat16)
        logits = jnp.einsum("cle,se->cls", u_bf16, emb_table, preferred_element_type=jnp.float32) + b_vocab
        local_max = jnp.max(logits, axis=-1)
        local_sum = jnp.sum(jnp.exp(logits - local_max[..., None]), axis=-1)
        is_label = (labels - row_start)[..., None] == jnp.arange(shard_rows)[None, None, :]
        label_logit = jnp.sum(jnp.where(is_label, logits, 0.0), axis=-1)
        tok_stats = lax.all_gather(jnp.stack([local_max, local_sum, label_logit]), "vp")
        global_max = jnp.max(tok_stats[:, 0], axis=0)
        log_norm = global_max + jnp.log(jnp.sum(tok_stats[:, 1] * jnp.exp(tok_stats[:, 0] - global_max), axis=0))
        target = jnp.sum(tok_stats[:, 2], axis=0)
        mlm_loss = lax.psum(jnp.sum(log_norm - target), "dp") / n_tokens
        d_logits = (jnp.exp(logits - log_norm[..., None]) - is_label.astype(jnp.float32)) / n_tokens
        d_logits_bf = d_logits.astype(jnp.bfloat16)
        d_emb_table = lax.psum(jnp.einsum("cls,cle->se", d_logits_bf, u_bf16, preferred_element_type=jnp.float32), "dp")
        d_b_vocab = lax.psum(jnp.sum(d_logits, axis=(0, 1)), "dp")
        du_part = jnp.einsum("cls,se->cle", d_logits_bf, emb_table, preferred_element_type=jnp.float32).astype(jnp.bfloat16)
        d_unorm = lax.psum(du_part.astype(jnp.float32), "vp")
        d_pre, d_ln_gain, d_ln_bias = head_vjp(d_unorm)
        d_pre_bf = d_pre.astype(jnp.bfloat16)
        d_w_trans = lax.psum(jnp.einsum("cle,clf->ef", masked_h, d_pre_bf, preferred_element_type=jnp.float32), "dp")
        vec_grads = lax.psum(jnp.stack([jnp.sum(d_pre, axis=(0, 1)), d_ln_gain, d_ln_bias]), "dp")
        d_masked = jnp.einsum("clf,ef->cle", d_pre_bf, w_trans, preferred_element_type=jnp.float32).astype(jnp.bfloat16)
        d_hidden = jnp.einsum("clt,cle->cte", pos_onehot, d_masked, preferred_element_type=jnp.float32).astype(jnp.bfloat16)
        return mlm_loss, d_hidden, d_w_trans, vec_grads[0], vec_grads[1], vec_grads[2], d_emb_table, d_b_vocab

    in_specs = (P("dp", None, None), P("dp", None), P("dp", None), P(None, None), P(None), P(None), P(None), P("vp", None), P("vp"))
    out_specs = (P(), P("dp", None, None), P(None, None), P(None), P(None), P(None), P("vp", None), P("vp"))
    return jax.shard_map(local_step, mesh=mesh, in_specs=in_specs, out_specs=out_specs, check_vma=False)
```

profile of v0, /device:TPU:1, one launch (start us, length us, event | category | flops | bytes accessed | tf_op | source)
XLA Modules:
  0.0 446.4 jit_solution(11855438703334231796)
XLA Ops:
  7.2 4.2 convolution_convert_fusion.1
  11.4 1.8 fusion.36
  13.2 6.1 %fusion.45 = (f32[6,77]{1,0:T(8,128)S(1)}, f32[6,77,1024]{2,1,0:T(8,128)S(1)}, f32[6,77,1024]{2,1,0:T(8,128)}) fusion(f32[6,77,1024]{2,1,0:T(8,128)S(1)} %get-tuple-element.30, f32[1024]{0:T(1024)S(1)} %copy-done.11, u8[77,1024]{1,0:T(8,128)(4,1)S(1)} %get-tuple-element.13, u8[77,1024]{1,0:T(8,128)(4,1)S(1)} %get-tuple-element.12), kind=kLoop, calls=%fused_computation.74 | loop fusion | flops 33588784 | bytes 5840696 | tf_op jit(solution)/shard_map/jvp()/reduce_sum | solution.py:11
  19.3 1.2 copy-done.1
  21.0 15.3 %fusion.48 = (f32[6,77]{1,0:T(8,128)S(1)}, f32[6,77,7648]{2,1,0:T(8,128)}) fusion(f32[7648]{0:T(1024)S(1)} %copy-done.13, bf16[7648,1024]{1,0:T(8,128)(2,1)} %param.16, f32[6,77,1024]{2,1,0:T(8,128)} %copy-done.1, f32[1024]{0:T(1024)S(1)} %copy-done.14, f32[1024]{0:T(1024)S(1)} %copy-done.10, f32[6,77]{1,0:T(8,128)S(1)} %fusion.41, ...), kind=kOutput, calls=%fused_computation.76 | convolution fusion | flops 7245785600 | bytes 31733288 | tf_op jit(solution)/shard_map/cle,se->cls/dot_general | solution.py:31
  36.3 7.7 %exponential_reduce_fusion = (f32[6,77]{1,0:T(8,128)S(1)}, f32[6,77]{1,0:T(8,128)S(1)}) fusion(f32[6,77,7648]{2,1,0:T(8,128)} %get-tuple-element.32, f32[6,77]{1,0:T(8,128)S(1)} %get-tuple-element.31, s32[6,77]{1,0:T(8,128)S(1)} %broadcast_subtract_fusion), kind=kLoop, calls=%fused_computation.8 | loop fusion | flops 17665956 | bytes 14140896 | tf_op jit(solution)/shard_map/reduce_sum | solution.py:33
  44.0 10.3 %all-gather = f32[12,6,77]{2,1,0:T(8,128)S(1)} all-gather(f32[3,6,77]{2,1,0:T(8,128)S(1)} %pad_maximum_fusion.1), channel_id=2, replica_groups=mesh['vp'=4,'dp'=32] {'vp'}, dimensions={0}, use_global_device_ids=true | all-gather | bytes 27720 | tf_op jit(solution)/shard_map/all_gather | solution.py:36
  54.4 0.6 subtract_reduce_fusion
  55.0 17.3 %fusion.22 = f32[6,77,1024]{2,1,0:T(8,128)} fusion(bf16[7648,1024]{1,0:T(8,128)(2,1)} %param.16, f32[6,77,7648]{2,1,0:T(8,128)} %get-tuple-element.32, f32[6,77]{1,0:T(8,128)S(1)} %get-tuple-element.23, s32[6,77]{1,0:T(8,128)S(1)} %broadcast_subtract_fusion), kind=kOutput, calls=%fused_computation.45 | convolution fusion | flops 7258500608 | bytes 31692656 | tf_op jit(solution)/shard_map/cls,se->cle/dot_general | solution.py:45
  72.3 20.6 %convolution_bitcast_fusion = f32[7648,1024]{1,0:T(8,128)} fusion(f32[6,77,1024]{2,1,0:T(8,128)} %copy-done.1, f32[1024]{0:T(1024)S(1)} %copy-done.14, f32[1024]{0:T(1024)S(1)} %copy-done.10, f32[6,77]{1,0:T(8,128)S(1)} %fusion.41, f32[6,77]{1,0:T(8,128)S(1)} %broadcast_multiply_fusion, f32[6,77,7648]{2,1,0:T(8,128)} %get-tuple-element.32, ...), kind=kOutput, calls=%fused_computation | convolution fusion | flops 7259919872 | bytes 47367648 | tf_op jit(solution)/shard_map/cls,cle->se/dot_general | solution.py:43
  93.0 40.2 %all-reduce.5.cloned.1.call-done = f32[6,77,1024]{2,1,0:T(8,128)} async-done(((f32[6,77,1024]{2,1,0:T(8,128)}), f32[6,77,1024]{2,1,0:T(8,128)}) %all-reduce.5.cloned.1.call-update) | async-done | bytes 1892368 | tf_op jit(solution)/shard_map/psum | solution.py:46
  133.2 2.7 multiply_reduce_fusion.1
  135.9 0.6 copy-done.3
  136.5 1.0 multiply_reduce_fusion
  138.0 0.6 copy-done.6
  138.6 1.6 fusion.44
  140.2 3.3 convolution_bitcast_fusion.1
  143.6 7.8 %fusion.7 = f32[7648]{0:T(1024)S(1)} fusion(f32[6,77,7648]{2,1,0:T(8,128)} %get-tuple-element.32, f32[6,77]{1,0:T(8,128)S(1)} %get-tuple-element.23, s32[6,77]{1,0:T(8,128)S(1)} %broadcast_subtract_fusion), kind=kLoop, calls=%fused_computation.10 | loop fusion | flops 21192608 | bytes 14167792 | tf_op jit(solution)/shard_map/reduce_sum | solution.py:44
  151.5 124.8 %all-reduce = (f32[]{:T(128)}, f32[3,1024]{1,0:T(4,128)S(1)}, f32[7648]{0:T(1024)}) all-reduce(f32[]{:T(128)} %get-tuple-element.22, f32[3,1024]{1,0:T(4,128)S(1)} %pad_maximum_fusion, f32[7648]{0:T(1024)S(1)} %fusion.7), channel_id=1, replica_groups=mesh['vp'=4,'dp'=32] {'dp'}, use_global_device_ids=true, to_apply=%region_9.10 | all-reduce | flops 10721 | bytes 85768 | tf_op jit(solution)/shard_map/psum | solution.py:40
  276.9 0.6 fusion.47
  277.5 4.8 %convolution_convert_fusion = bf16[6,512,1024]{2,1,0:T(8,128)(2,1)} fusion(bf16[1024,1024]{1,0:T(8,128)(2,1)S(1)} %copy-done, bf16[6,77,1024]{2,1,0:T(8,128)(2,1)S(1)} %get-tuple-element.21, s32[6,77]{1,0:T(8,128)S(1)} %copy-done.9), kind=kOutput, calls=%fused_computation.12 | convolution fusion | flops 1457181696 | bytes 9336632 | tf_op jit(solution)/shard_map/clt,cle->cte/dot_general | solution.py:52
  282.3 129.2 %all-reduce.7.cloned.1.call-done = (f32[1024,1024]{1,0:T(8,128)}, f32[7648,1024]{1,0:T(8,128)}) async-done(((f32[1024,1024]{1,0:T(8,128)}, f32[7648,1024]{1,0:T(8,128)}), (f32[1024,1024]{1,0:T(8,128)}, f32[7648,1024]{1,0:T(8,128)})) %all-reduce.7.cloned.1.call-update) | async-done | bytes 35520528 | tf_op jit(solution)/shard_map/psum | solution.py:49
  411.5 4.8 %copy.23 = f32[1024,1024]{1,0:T(8,128)} copy(f32[1024,1024]{1,0:T(8,128)} %get-tuple-element.37) | data formatting | bytes 8388608
  416.3 22.1 %copy.24 = f32[7648,1024]{1,0:T(8,128)} copy(f32[7648,1024]{1,0:T(8,128)} %get-tuple-element.41) | data formatting | bytes 62652416
  (42 shorter events, 1.1 us)
Async XLA Ops:
  7.2 4.3 copy-start
  7.2 126.0 %all-reduce.5.cloned.1.call-start = ((), (), s32[]{:S(2)}) async-start(), calls=%async_computation | async-start | bytes 3932160 | tf_op jit(solution)/shard_map/psum | solution.py:46
  7.2 4.2 copy-start.11
  11.4 1.8 copy-start.7
  13.2 6.1 %copy-start.4 = (f32[6,77,1024]{2,1,0:T(8,128)}, f32[6,77,1024]{2,1,0:T(8,128)S(1)}, u32[]{:S(2)}) copy-start(f32[6,77,1024]{2,1,0:T(8,128)S(1)} %get-tuple-element.30) | copy-start | bytes 5677060
  19.3 1.3 copy-start.1
  19.3 1.6 copy-start.12
  19.3 1.7 copy-start.10
  19.3 1.7 copy-start.13
  19.3 1.7 copy-start.14
  72.3 339.2 %all-reduce.7.cloned.1.call-start = ((), (), s32[]{:S(2)}) async-start(), calls=%async_computation.1 | async-start | bytes 71041024 | tf_op jit(solution)/shard_map/psum | solution.py:49
  133.2 2.7 copy-start.2
  133.2 3.3 copy-start.3
  136.5 1.5 copy-start.5
  136.5 2.1 copy-start.6
  138.6 1.6 copy-start.8
  143.6 133.9 %copy-start.9 = (s32[6,77]{1,0:T(8,128)S(1)}, s32[6,77]{1,0:T(8,128)}, u32[]{:S(2)}) copy-start(s32[6,77]{1,0:T(8,128)} %param.10) | copy-start | bytes 5548
Sparse Core Ops, SparseCore 0:
  72.4 60.7 all-reduce.4
  143.7 267.7 all-reduce.6
where the time goes:
time: 447 us; the launch traced here: 446 us
  waiting for transfers between devices  169 us (38%)
  blocking collectives  135 us (30%)
  matrix products  67.3 us (15%)
  local copies, waits for them, and re-layouts  30.5 us (7%)
  other arithmetic  28 us (6%)
  between operations  16.1 us (4%)
    psum x1, waiting for transfers between devices, local_step(): lax.psum(jnp.einsum('cle,clf->ef', masked_h, d_pre_bf, preferred_element_...  129 us
    psum x1, blocking collectives, local_step(): mlm_loss = lax.psum(jnp.sum(log_norm - target), 'dp') / n_tokens  125 us
    psum x1, waiting for transfers between devices, local_step(): d_unorm = lax.psum(du_part.astype(jnp.float32), 'vp')  40.2 us
    unnamed x32, local copies, waits for them, and re-layouts  29.9 us
    dot_general x1, matrix products, local_step(): jnp.einsum('cls,cle->se', d_logits_bf, u_bf16, preferred_element_type=jnp...  20.6 us
    dot_general x1, matrix products, local_step(): jnp.einsum('cls,se->cle', d_logits_bf, emb_table, preferred_element_type=...  17.3 us
    dot_general x1, matrix products, local_step(): jnp.einsum('cle,se->cls', u_bf16, emb_table, preferred_element_type=jnp.f...  15.3 us
    all_gather x1, blocking collectives, local_step(): lax.all_gather(jnp.stack([local_max, local_sum, label_logit]), 'vp')  10.3 us
  transfers between devices with their start and end apart: 2, of which 2 were waited for; matrix products, arithmetic and copies ran while one was open for 8% of the time, Pallas kernels for 0%

commit v1 on v0

v1 whole, which is shorter than its diff:
```python
import functools

import jax
import jax.numpy as jnp
from jax import lax
from jax.experimental import pallas as pl
from jax.experimental.pallas import tpu as pltpu
from jax.sharding import PartitionSpec as P

MESH = pl.DeviceIdType.MESH
LN_EPS = 1e-5
TOK = 512
VROWS = 3824
NCH = 8
ROWS = 3840
HALF = 1920
SH = 480
SUB = 120
BLK = 384

def add_rows(dst, k, d0, srcs, n, blk):
    def body(i, c):
        o = pl.multiple_of(i * blk, 8)
        v = dst[k, pl.ds(pl.multiple_of(d0 + o, 8), blk), :]
        for s in srcs:
            v = v + s[pl.ds(o, blk), :]
        dst[k, pl.ds(pl.multiple_of(d0 + o, 8), blk), :] = v
        return c
    lax.fori_loop(0, n // blk, body, 0)


def reduce_kernel(gt, u, both, r1, r2, r3, r4, a1, a2, ssem, rsem, psend, precv):
    m, oth = both.at[0], both.at[1]
    dp = lax.axis_index("dp")
    z, y, c = dp // 8, (dp // 2) % 4, dp % 2
    ynb = [z * 8 + ((y + d) % 4) * 2 + c for d in (1, 3)]
    znb = [((z + d) % 4) * 8 + y * 2 + c for d in (1, 3)]
    mate = dp + 1 - 2 * c
    barrier = pltpu.get_barrier_semaphore()
    for d in ynb + znb + [mate]:
        pl.semaphore_signal(barrier, inc=1, device_id={"dp": d}, device_id_type=MESH)
    pl.semaphore_wait(barrier, 5)
    halves = ((0, y, ynb, z, znb), (HALF, z, znb, y, ynb))

    def copy(src, dst, st, h, d, k, dev):
        return pltpu.make_async_remote_copy(
            src_ref=src, dst_ref=dst, send_sem=ssem.at[st, h, d, k], recv_sem=rsem.at[st, h, d, k],
            device_id={"dp": dev}, device_id_type=MESH)

    def rows(k, start, n):
        return m.at[k, pl.ds(pl.multiple_of(start, 8), n)]

    def stage_copies(st, k):
        out = []
        for h, (b, p, pn, q, qn) in enumerate(halves):
            b2 = b + p * SH
            op, oq = (p + 2) % 4, (q + 2) % 4
            pp, pm, qp, qm = (p + 1) % 4, (p + 3) % 4, (q + 1) % 4, (q + 3) % 4
            if st == 0:
                a = rows(k, b + op * SH, 240), r1.at[k % 2, h, 0], rows(k, b + op * SH + 240, 240), r1.at[k % 2, h, 1], pn
            elif st == 1:
                a = rows(k, b + pp * SH, SH), r2.at[k % 2, h, 0], rows(k, b + pm * SH, SH), r2.at[k % 2, h, 1], pn
            elif st == 2:
                a = (rows(k, b2 + oq * SUB, 64), r3.at[k % 2, h, 0], rows(k, b2 + oq * SUB + 64, 56),
                     r3.at[k % 2, h, 1, pl.ds(0, 56)], qn)
            elif st == 3:
                a = rows(k, b2 + qp * SUB, SUB), r4.at[k % 2, h, 0], rows(k, b2 + qm * SUB, SUB), r4.at[k % 2, h, 1], qn
            elif st == 4:
                s = rows(k, b2 + q * SUB, SUB)
                a = s, a1.at[k % 3, h, 0], s, a1.at[k % 3, h, 1], qn
            elif st == 5:
                a = (a1.at[k % 3, h, 0, pl.ds(0, 64)], a2.at[k % 3, h, 0], a1.at[k % 3, h, 1, pl.ds(64, 56)],
                     a2.at[k % 3, h, 1, pl.ds(0, 56)], qn)
            elif st == 6:
                s = rows(k, b2, SH)
                a = s, s, s, s, pn
            else:
                s0, s1 = rows(k, b + pm * SH, 240), rows(k, b + pp * SH + 240, 240)
                a = s0, s0, s1, s1, pn
            out.append(copy(a[0], a[1], st, h, 0, k, a[4][0]))
            out.append(copy(a[2], a[3], st, h, 1, k, a[4][1]))
        return out

    def mate_copy(k):
        return pltpu.make_async_remote_copy(
            src_ref=m.at[k], dst_ref=oth.at[k], send_sem=psend.at[k], recv_sem=precv.at[k],
            device_id={"dp": mate}, device_id_type=MESH)

    def stage(st, k):
        if st == 0:
            def mm(i, cc):
                o = pl.multiple_of(i * SH, 8)
                m[k, pl.ds(o, SH), :] = jnp.dot(gt[pl.ds(o, SH), :], u[:, pl.ds(pl.multiple_of(k * 128, 128), 128)], preferred_element_type=jnp.float32)
                return cc
            lax.fori_loop(0, ROWS // SH, mm, 0)
        else:
            for cp in stage_copies(st - 1, k):
                cp.wait()
            for h, (b, p, pn, q, qn) in enumerate(halves):
                b2 = b + p * SH
                pp, pm, qp, qm = (p + 1) % 4, (p + 3) % 4, (q + 1) % 4, (q + 3) % 4
                if st == 1:
                    add_rows(m, k, b + pp * SH, [r1.at[k % 2, h, 0]], 240, 80)
                    add_rows(m, k, b + pm * SH + 240, [r1.at[k % 2, h, 1]], 240, 80)
                elif st == 2:
                    add_rows(m, k, b2, [r2.at[k % 2, h, 0], r2.at[k % 2, h, 1]], SH, 80)
                elif st == 3:
                    add_rows(m, k, b2 + qp * SUB, [r3.at[k % 2, h, 0]], 64, 64)
                    add_rows(m, k, b2 + qm * SUB + 64, [r3.at[k % 2, h, 1]], 56, 56)
                elif st == 4:
                    add_rows(m, k, b2 + q * SUB, [r4.at[k % 2, h, 0], r4.at[k % 2, h, 1]], SUB, 40)
                elif st == 5:
                    rows(k, b2 + qm * SUB, SUB)[...] = a1[k % 3, h, 0]
                    rows(k, b2 + qp * SUB, SUB)[...] = a1[k % 3, h, 1]
                elif st == 6:
                    oq = (q + 2) % 4
                    rows(k, b2 + oq * SUB, 64)[...] = a2[k % 3, h, 0]
                    rows(k, b2 + oq * SUB + 64, 56)[...] = a2[k % 3, h, 1, pl.ds(0, 56)]
        if st < 8:
            for cp in stage_copies(st, k):
                cp.start()
        else:
            mate_copy(k).start()

    def step(t, carry):
        for st in range(8, -1, -1):
            k = t - st

            @pl.when((k >= 0) & (k < NCH))
            def _():
                stage(st, k)
        return carry

    lax.fori_loop(0, NCH + 8, step, 0)

    def drain(k, carry):
        mate_copy(k).wait()
        return carry

    lax.fori_loop(0, NCH, drain, 0)


def reduce_call(gt, u):
    f32 = jnp.float32
    vm = pl.BlockSpec(memory_space=pltpu.VMEM)
    return pl.pallas_call(
        reduce_kernel,
        out_shape=pltpu.VMEM((2, NCH, ROWS, 128), f32),
        in_specs=[vm, vm],
        out_specs=vm,
        scratch_shapes=[
            pltpu.VMEM((2, 2, 2, 240, 128), f32), pltpu.VMEM((2, 2, 2, SH, 128), f32),
            pltpu.VMEM((2, 2, 2, 64, 128), f32), pltpu.VMEM((2, 2, 2, SUB, 128), f32),
            pltpu.VMEM((3, 2, 2, SUB, 128), f32), pltpu.VMEM((3, 2, 2, 64, 128), f32),
            pltpu.SemaphoreType.DMA((8, 2, 2, NCH)), pltpu.SemaphoreType.DMA((8, 2, 2, NCH)),
            pltpu.SemaphoreType.DMA((NCH,)), pltpu.SemaphoreType.DMA((NCH,)),
        ],
        compiler_params=pltpu.CompilerParams(collective_id=1, has_side_effects=True, vmem_limit_bytes=20 << 20),
        name="reduce_rows",
    )(gt, u)


def write_kernel(both, out, sem):
    c = lax.axis_index("dp") % 2
    cps = []
    for k in range(NCH):
        for j, src in enumerate((both.at[0], both.at[1])):
            r0 = (c if j == 0 else 1 - c) * 3824
            cp = pltpu.make_async_copy(src.at[k, pl.ds(0, 3824)],
                                       out.at[pl.ds(pl.multiple_of(r0, 8), 3824), pl.ds(k * 128, 128)], sem.at[k, j])
            cp.start()
            cps.append(cp)
    for cp in cps:
        cp.wait()


def write_call(both):
    vm = pl.BlockSpec(memory_space=pltpu.VMEM)
    return pl.pallas_call(
        write_kernel,
        out_shape=jax.ShapeDtypeStruct((7648, 1024), jnp.float32),
        in_specs=[vm],
        out_specs=pl.BlockSpec(memory_space=pl.ANY),
        scratch_shapes=[pltpu.SemaphoreType.DMA((NCH, 2))],
        compiler_params=pltpu.CompilerParams(vmem_limit_bytes=1 << 20),
        name="write_rows",
    )(both)


def head_norm(pre_act, ln_gain, ln_bias):
    gelu_out = jax.nn.gelu(pre_act, approximate=False)
    row_mean = jnp.mean(gelu_out, axis=-1, keepdims=True)
    centered = gelu_out - row_mean
    row_var = jnp.mean(centered * centered, axis=-1, keepdims=True)
    return centered * lax.rsqrt(row_var + LN_EPS) * ln_gain + ln_bias


def column(row):
    return jnp.transpose(jnp.broadcast_to(row, (128, 128)))


def softmax_kernel(n_valid, scale, u_own, lab_own, bias, emb, gt, u_all, small,
                   emb_v, logit, u_rx, lab_rx, stat, stats, sem_e, sem_s, sem_r, st_s, st_r):
    f32 = jnp.float32
    dp, vp = lax.axis_index("dp"), lax.axis_index("vp")
    c = dp % 2
    mate = dp + 1 - 2 * c
    peers = [(dx, dc) for dx in range(4) for dc in range(2) if (dx, dc) != (0, 0)]

    def peer(dx, dc):
        return {"vp": (vp + dx) % 4, "dp": (dp // 2) * 2 + (c + dc) % 2}

    barrier = pltpu.get_barrier_semaphore()
    for dx, dc in peers:
        pl.semaphore_signal(barrier, inc=1, device_id=peer(dx, dc), device_id_type=MESH)

    def load(i, n):
        r0 = pl.multiple_of(c * VROWS, 16) + i * BLK
        return pltpu.make_async_copy(emb.at[pl.ds(r0, n)], emb_v.at[pl.ds(i * BLK, n)], sem_e.at[i])

    n_blk = ROWS // BLK
    last = VROWS - (n_blk - 1) * BLK
    for i in range(n_blk):
        load(i, BLK if i < n_blk - 1 else last).start()
    emb_v[pl.ds(VROWS, ROWS - VROWS), :] = jnp.zeros((ROWS - VROWS, 1024), jnp.bfloat16)
    own0 = pl.multiple_of(c * TOK, TOK)
    oth0 = pl.multiple_of((1 - c) * TOK, TOK)
    u_all[pl.ds(own0, TOK), :] = u_own[...].astype(jnp.bfloat16)
    pl.semaphore_wait(barrier, len(peers))
    cp_u = pltpu.make_async_remote_copy(src_ref=u_own, dst_ref=u_rx, send_sem=sem_s.at[0], recv_sem=sem_r.at[0],
                                        device_id={"dp": mate}, device_id_type=MESH)
    cp_l = pltpu.make_async_remote_copy(src_ref=lab_own, dst_ref=lab_rx, send_sem=sem_s.at[1], recv_sem=sem_r.at[1],
                                        device_id={"dp": mate}, device_id_type=MESH)
    cp_u.start()
    cp_l.start()
    row0 = (vp * 2 * VROWS + c * VROWS).astype(f32)

    def local_labels(ref):
        v = ref[0:1, :] - row0
        return jnp.where((v >= 0) & (v < VROWS), v, -1.0)

    def half_logits(tok0, lab):
        u = u_all[pl.ds(tok0, TOK), :]
        labs = jnp.broadcast_to(lab, (8, TOK))
        sub = lax.broadcasted_iota(jnp.int32, (8, TOK), 0).astype(f32)

        def block(i, carry):
            mx, sm, lb = carry
            e = emb_v[pl.ds(pl.multiple_of(i * BLK, BLK), BLK), :]
            x = lax.dot_general(e, u, (((1,), (1,)), ((), ())), preferred_element_type=f32)
            b = jnp.concatenate([column(bias[pl.ds(i * 3 + j, 1), :]) for j in range(BLK // 128)], axis=0)
            x = x + jnp.concatenate([b] * (TOK // 128), axis=1)
            logit[pl.ds(pl.multiple_of(i * BLK, BLK), BLK), pl.ds(tok0, TOK)] = x
            x = x.reshape(BLK // 8, 8, TOK)
            top = jnp.maximum(mx, jnp.max(x, axis=0))
            sm = sm * jnp.exp(mx - top) + jnp.sum(jnp.exp(x - top[None]), axis=0)
            rel = labs - sub - (i * BLK).astype(f32)
            ids = (lax.broadcasted_iota(jnp.int32, (BLK // 8, 8, TOK), 0) * 8).astype(f32)
            lb = lb + jnp.sum(jnp.where(ids == rel[None], x, 0.0), axis=0)
            return top, sm, lb

        init = (jnp.full((8, TOK), -3e38, f32), jnp.zeros((8, TOK), f32), jnp.zeros((8, TOK), f32))
        mx, sm, lb = lax.fori_loop(0, n_blk, block, init)
        top = jnp.max(mx, axis=0, keepdims=True)
        sm = jnp.sum(sm * jnp.exp(mx - top), axis=0, keepdims=True)
        lb = jnp.sum(lb, axis=0, keepdims=True)
        stat[:, pl.ds(tok0, TOK)] = jnp.concatenate([top, sm, lb, jnp.zeros((5, TOK), f32)], axis=0)

    for i in range(n_blk):
        load(i, BLK if i < n_blk - 1 else last).wait()
    lab1 = local_labels(lab_own)
    half_logits(own0, lab1)
    cp_u.wait()
    cp_l.wait()
    u_all[pl.ds(oth0, TOK), :] = u_rx[...].astype(jnp.bfloat16)
    lab2 = local_labels(lab_rx)
    half_logits(oth0, lab2)
    cps = [pltpu.make_async_remote_copy(src_ref=stat, dst_ref=stats.at[j], send_sem=st_s.at[j], recv_sem=st_r.at[j],
                                        device_id=peer(dx, dc), device_id_type=MESH)
           for j, (dx, dc) in enumerate(peers)]
    for cp in cps:
        cp.start()
    for cp in cps:
        cp.wait()
    mine = stat[...]
    top = mine[0:1]
    for j in range(len(peers)):
        top = jnp.maximum(top, stats[j, 0:1, :])
    tot = mine[1:2] * jnp.exp(mine[0:1] - top)
    tgt = mine[2:3]
    for j in range(len(peers)):
        tot = tot + stats[j, 1:2, :] * jnp.exp(stats[j, 0:1, :] - top)
        tgt = tgt + stats[j, 2:3, :]
    norm = top + jnp.log(tot)
    lane = lax.broadcasted_iota(jnp.int32, (1, 2 * TOK), 1)
    valid = (lane % TOK) < n_valid
    diff = jnp.where(valid, norm - tgt, 0.0)
    own_lane = (lane // TOK) == c
    diff = jnp.where(own_lane, diff, 0.0)
    small[30:31, :] = sum(diff[:, j * 128:(j + 1) * 128] for j in range(8))
    norm = jnp.where(valid, norm, 3e38)
    stat[0:1, :] = norm
    stat[1:2, pl.ds(own0, TOK)] = lab1
    stat[1:2, pl.ds(oth0, TOK)] = lab2

    def grad(i, carry):
        r = pl.multiple_of(i * 128, 128)
        x = logit[pl.ds(r, 128), :]
        ids = (lax.broadcasted_iota(jnp.int32, (128, 2 * TOK), 0) + i * 128).astype(f32)
        g = (jnp.exp(x - stat[0:1, :]) - jnp.where(ids == stat[1:2, :], 1.0, 0.0)) * scale
        gt[pl.ds(r, 128), :] = g.astype(jnp.bfloat16)
        s = sum(g[:, j * 128:(j + 1) * 128] for j in range(8))
        small[pl.ds(i, 1), :] = jnp.sum(jnp.transpose(s), axis=0, keepdims=True)
        return carry

    lax.fori_loop(0, ROWS // 128, grad, 0)


def softmax_call(n_valid, scale, u_own, lab_own, bias, emb):

    f32, bf = jnp.float32, jnp.bfloat16
    vm = pl.BlockSpec(memory_space=pltpu.VMEM)
    dma = pltpu.SemaphoreType.DMA
    return pl.pallas_call(
        functools.partial(softmax_kernel, n_valid, scale),
        out_shape=(pltpu.VMEM((ROWS, 2 * TOK), bf), pltpu.VMEM((2 * TOK, 1024), bf), pltpu.VMEM((32, 128), f32)),
        in_specs=[vm, vm, vm, pl.BlockSpec(memory_space=pl.ANY)],
        out_specs=(vm, vm, vm),
        scratch_shapes=[
            pltpu.VMEM((ROWS, 1024), bf), pltpu.VMEM((ROWS, 2 * TOK), f32), pltpu.VMEM((TOK, 1024), f32),
            pltpu.VMEM((8, TOK), f32), pltpu.VMEM((8, 2 * TOK), f32), pltpu.VMEM((7, 8, 2 * TOK), f32),
            dma((ROWS // BLK,)), dma((2,)), dma((2,)), dma((7,)), dma((7,)),
        ],
        compiler_params=pltpu.CompilerParams(collective_id=0, has_side_effects=True, vmem_limit_bytes=44 << 20),
        name="softmax_rows",
    )(u_own, lab_own, bias, emb)


def solution(mesh):
    n_groups = mesh.shape["dp"]
    f32, bf = jnp.float32, jnp.bfloat16

    def local_step(hidden, mask_pos, labels, w_trans, b_trans, ln_gain, ln_bias, emb_table, b_vocab):
        n_rows, seq_len = hidden.shape[0], hidden.shape[1]
        n_masks = mask_pos.shape[1]
        n_own = n_rows * n_masks
        n_tokens = n_own * n_groups
        dp, vp = lax.axis_index("dp"), lax.axis_index("vp")
        c = dp % 2
        pos_onehot = (mask_pos[:, :, None] == jnp.arange(seq_len)[None, None, :]).astype(bf)
        masked_h = jnp.einsum("clt,cte->cle", pos_onehot, hidden, preferred_element_type=f32).astype(bf)
        masked_h = jnp.pad(masked_h.reshape(n_own, 1024), ((0, TOK - n_own), (0, 0)))
        pre_act = jnp.dot(masked_h, w_trans, preferred_element_type=f32) + b_trans
        u_norm, head_vjp = jax.vjp(head_norm, pre_act, ln_gain, ln_bias)
        u_own = u_norm.astype(bf).astype(f32)
        lab = jnp.pad(labels.reshape(n_own).astype(f32), (0, TOK - n_own), constant_values=-1e6)
        lab = jnp.broadcast_to(lab[None], (8, TOK))
        b_half = lax.dynamic_slice(b_vocab, (c * VROWS,), (VROWS,))
        bias = jnp.pad(b_half, (0, ROWS - VROWS), constant_values=-3e38).reshape(ROWS // 128, 128)
        gt, u_all, small = softmax_call(n_own, 1.0 / n_tokens, u_own, lab, bias, emb_table)
        emb_half = lax.dynamic_slice(emb_table, (c * VROWS, 0), (VROWS, 1024))
        du = lax.dot_general(gt[:VROWS], emb_half, (((0,), (0,)), ((), ())), preferred_element_type=f32)
        perm = [(i, i ^ 1) for i in range(n_groups)]
        du_mine = lax.dynamic_slice(du, (c * TOK, 0), (TOK, 1024))
        du_theirs = lax.dynamic_slice(du, ((1 - c) * TOK, 0), (TOK, 1024))
        du_block = (du_mine + lax.ppermute(du_theirs, "dp", perm)).astype(bf)
        d_unorm = lax.psum(du_block.astype(f32), "vp")
        d_pre, d_ln_gain, d_ln_bias = head_vjp(d_unorm)
        d_pre_bf = d_pre.astype(bf)
        h_part = lax.dynamic_slice(masked_h, (0, vp * 256), (TOK, 256))
        dw_part = lax.dot_general(h_part, d_pre_bf, (((0,), (0,)), ((), ())), preferred_element_type=f32)
        d_b = lax.dynamic_update_slice(jnp.zeros((8192,), f32), small[:30].reshape(ROWS)[:VROWS], (c * VROWS,)).reshape(8, 1024)
        loss = jnp.broadcast_to(jnp.sum(small[30]) / n_tokens, (1, 1024))
        packed = jnp.concatenate([dw_part, d_b, jnp.stack([jnp.sum(d_pre, axis=0), d_ln_gain, d_ln_bias]), loss], axis=0)
        packed = lax.psum(packed, "dp")
        d_w_trans = lax.all_gather(packed[:256], "vp", tiled=True)
        d_masked = jnp.dot(d_pre_bf, w_trans.T, preferred_element_type=f32).astype(bf)[:n_own].reshape(n_rows, n_masks, 1024)
        d_hidden = jnp.einsum("clt,cle->cte", pos_onehot, d_masked, preferred_element_type=f32).astype(bf)
        d_emb = write_call(reduce_call(gt, u_all))
        d_b_vocab = packed[256:264].reshape(8192)[:2 * VROWS]
        return packed[267, 0], d_hidden, d_w_trans, packed[264], packed[265], packed[266], d_emb, d_b_vocab

    in_specs = (P("dp", None, None), P("dp", None), P("dp", None), P(None, None), P(None), P(None), P(None), P("vp", None), P("vp"))
    out_specs = (P(), P("dp", None, None), P(None, None), P(None), P(None), P(None), P("vp", None), P("vp"))
    return jax.shard_map(local_step, mesh=mesh, in_specs=in_specs, out_specs=out_specs, check_vma=False)
```

time: 447 us -> 492 us (1.10)
  Pallas kernels: 0 us -> 232 us
  blocking collectives: 135 us -> 0 us
  matrix products: 67.3 us -> 31.9 us
  other arithmetic: 28 us -> 13.3 us
    pallas_call x0 -> x3, Pallas kernels: none -> 232 us  [the longest x1 186 us: reduce_call(): pl.pallas_call(reduce_kernel, out_shape=pltpu.VMEM((2, NCH, ROWS, 128), f...]
    psum x1 -> x0, blocking collectives: 125 us -> none  [local_step(): mlm_loss = lax.psum(jnp.sum(log_norm - target), 'dp') / n_tokens]
    dot_general x7 -> x6, matrix products: 67.3 us -> 31.9 us  [the longest x1 11.9 us: local_step(): lax.dot_general(gt[:VROWS], emb_half, (((0,), (0,)), ((), ())), preferred...]
    reduce_sum x7 -> x2, other arithmetic: 23.9 us -> 2.4 us  [the longest x1 1.8 us: local_step(): jnp.sum(d_pre, axis=0)]
    unnamed x32 -> x31, local copies, waits for them, and re-layouts: 29.9 us -> 14.5 us
    all_gather x1 -> x0, blocking collectives: 10.3 us -> none  [local_step(): lax.all_gather(jnp.stack([local_max, local_sum, label_logit]), 'vp')]
    convert_element_type x0 -> x3, other arithmetic: none -> 6.71 us  [the longest x1 4.17 us: local_step(): d_unorm = lax.psum(du_block.astype(f32), 'vp')]
    psum x2, waiting for transfers between devices: 169 us -> 163 us  [the longest x1 106 us: local_step(): packed = lax.psum(packed, 'dp')]
  transfers between devices with their start and end apart: 2 -> 4, of which waited for: 2 -> 3; matrix products, arithmetic and copies ran while one was open for 8% -> 3% of each run, Pallas kernels for 0% -> 40%
where the time goes in v1:
time: 492 us
  Pallas kernels  232 us (47%)
  waiting for transfers between devices  167 us (34%)
  local copies, waits for them, and re-layouts  32.3 us (7%)
  matrix products  31.9 us (6%)
  between operations  14.6 us (3%)
  other arithmetic  13.3 us (3%)
    pallas_call x1, Pallas kernels, reduce_call(): pl.pallas_call(reduce_kernel, out_shape=pltpu.VMEM((2, NCH, ROWS, 128), f...  186 us
    psum x1, waiting for transfers between devices, local_step(): packed = lax.psum(packed, 'dp')  106 us
    psum x1, waiting for transfers between devices, local_step(): d_unorm = lax.psum(du_block.astype(f32), 'vp')  56.9 us
    pallas_call x1, Pallas kernels, softmax_call(): pl.pallas_call(functools.partial(softmax_kernel, n_valid, scale), out_sha...  35.4 us
    unnamed x31, local copies, waits for them, and re-layouts  14.5 us
    dot_general x1, matrix products, local_step(): lax.dot_general(gt[:VROWS], emb_half, (((0,), (0,)), ((), ())), preferred...  11.9 us
    pallas_call x1, Pallas kernels, write_call(): pl.pallas_call(write_kernel, out_shape=jax.ShapeDtypeStruct((7648, 1024),...  10.4 us
  transfers between devices with their start and end apart: 4, of which 3 were waited for; matrix products, arithmetic and copies ran while one was open for 3% of the time, Pallas kernels for 40%

profile of v1, /device:TPU:1, one launch (start us, length us, event | category | flops | bytes accessed | tf_op | source)
XLA Modules:
  0.0 491.6 jit_solution(11082787162861760933)
XLA Ops:
  9.0 4.1 convolution_convert_fusion.1
  14.3 8.5 %fusion.27 = (f32[512]{0:T(512)S(1)}, f32[512,1024]{1,0:T(8,128)S(1)}, f32[512,1024]{1,0:T(8,128)}, f32[512,1024]{1,0:T(8,128)}) fusion(f32[1024]{0:T(1024)S(1)} %copy-done.13, bf16[1024,1024]{1,0:T(8,128)(2,1)S(1)} %copy-done, bf16[462,1024]{1,0:T(8,128)(2,1)} %reshape.75), kind=kOutput, calls=%fused_computation.60 | convolution fusion | flops 1108344320 | bytes 9340928 | tf_op jit(solution)/shard_map/dot_general | solution.py:353
  23.5 1.7 fusion.9.u_own
  25.2 35.4 %softmax_rows.1 = (bf16[3840,1024]{1,0:T(8,128)(2,1)S(1)}, bf16[1024,1024]{1,0:T(8,128)(2,1)S(1)}, f32[32,128]{1,0:T(8,128)S(1)}) custom-call(f32[512,1024]{1,0:T(8,128)} %fusion.9.u_own, f32[8,512]{1,0:T(8,128)S(1)} %broadcast_in_dim.10.lab_own, f32[30,128]{1,0:T(8,128)S(1)} %pad_bitcast_fusion.bias, bf16[7648,1024]{1,0:T(8,128)(2,1)} %emb.1), custom_call_target="tpu_custom_call" | custom-call | tf_op jit(solution)/shard_map/softmax_rows/pallas_call | solution.py:324
  60.6 1.3 copy-done.2
  62.0 3.2 copy-done.1
  65.2 11.9 %fusion = f32[1024,1024]{1,0:T(8,128)} fusion(bf16[7648,1024]{1,0:T(8,128)(2,1)} %emb.1, s32[]{:T(128)S(6)} %select_n.25, bf16[3840,1024]{1,0:T(8,128)(2,1)S(1)} %get-tuple-element.11.gt), kind=kOutput, calls=%fused_computation | convolution fusion | flops 8019509248 | bytes 19857412 | tf_op jit(solution)/shard_map/dot_general | solution.py:362
  77.1 3.2 constant_dynamic-slice_fusion
  80.7 3.8 collective-permute-done
  84.5 4.2 fusion.10
  90.4 56.9 %all-reduce.6.cloned.1.call-done = f32[512,1024]{1,0:T(8,128)} async-done(((f32[512,1024]{1,0:T(8,128)}), f32[512,1024]{1,0:T(8,128)}) %all-reduce.6.cloned.1.call-update) | async-done | bytes 2097168 | tf_op jit(solution)/shard_map/psum | solution.py:367
  147.2 2.9 fusion.25
  152.9 1.8 fusion.26
  154.8 1.5 fusion.16
  156.2 4.6 concatenate.3
  160.9 106.1 %all-reduce.8.cloned.1.call-done = f32[268,1024]{1,0:T(8,128)} async-done(((f32[268,1024]{1,0:T(8,128)}), f32[268,1024]{1,0:T(8,128)}) %all-reduce.8.cloned.1.call-update) | async-done | bytes 1097744 | tf_op jit(solution)/shard_map/psum | solution.py:375
  267.0 2.3 slice.51
  269.3 1.6 copy-done.3
  270.9 186.5 %reduce_rows.1.both = f32[2,8,3840,128]{3,2,1,0:T(8,128)S(1)} custom-call(bf16[3840,1024]{1,0:T(8,128)(2,1)} %copy-done.1, bf16[1024,1024]{1,0:T(8,128)(2,1)S(1)} %copy-done.3), custom_call_target="tpu_custom_call" | custom-call | tf_op jit(solution)/shard_map/reduce_rows/pallas_call | solution.py:146
  457.4 10.4 %write_rows.1 = f32[7648,1024]{1,0:T(8,128)} custom-call(f32[2,8,3840,128]{3,2,1,0:T(8,128)S(1)} %reduce_rows.1.both), custom_call_target="tpu_custom_call" | custom-call | tf_op jit(solution)/shard_map/write_rows/pallas_call | solution.py:179
  470.1 1.5 reshape.81
  471.6 4.6 convolution_convert_fusion
  478.8 1.5 fusion.29
  480.3 4.8 copy.24
  (57 shorter events, 12.8 us)
Async XLA Ops:
  7.2 7.1 %copy-start = (bf16[1024,1024]{1,0:T(8,128)(2,1)S(1)}, bf16[1024,1024]{1,0:T(8,128)(2,1)}, u32[]{:S(2)}) copy-start(bf16[1024,1024]{1,0:T(8,128)(2,1)} %param.12) | copy-start | bytes 6291460
  7.2 140.1 %all-reduce.6.cloned.1.call-start = ((), (), s32[]{:S(2)}) async-start(), calls=%async_computation | async-start | bytes 4194304 | tf_op jit(solution)/shard_map/psum | solution.py:367
  9.0 5.3 %copy-start.13 = (f32[1024]{0:T(1024)S(1)}, f32[1024]{0:T(1024)}, u32[]{:S(2)}) copy-start(f32[1024]{0:T(1024)} %param.13) | copy-start | bytes 12292
  22.7 2.5 copy-start.4
  22.7 0.7 copy-start.11
  22.7 0.7 copy-start.12
  60.6 1.3 copy-start.2
  62.0 3.2 copy-start.1
  80.3 4.1 collective-permute-start
  88.7 178.3 %all-reduce.8.cloned.1.call-start = ((), (), s32[]{:S(2)}) async-start(), calls=%async_computation.1 | async-start | bytes 2228224 | tf_op jit(solution)/shard_map/psum | solution.py:375
  147.2 2.9 copy-start.5
  147.2 3.5 copy-start.6
  150.7 1.6 copy-start.8
  150.7 2.2 copy-start.9
  152.9 1.8 copy-start.7
  160.9 319.4 %all-gather.2.cloned.1.call-start = ((), (), s32[]{:S(2)}) async-start(), calls=%async_computation.2 | async-start | bytes 5242880 | tf_op jit(solution)/shard_map/all_gather | solution.py:376
  269.3 1.6 copy-start.3
  469.1 2.5 copy-start.10
Sparse Core Ops, SparseCore 0:
  88.8 58.3 all-reduce.5
  161.0 105.9 all-reduce.7
  269.4 47.1 all-gather.1

commit v2 on v0

v2 whole, which is shorter than its diff:
```python
import functools

import jax
import jax.numpy as jnp
from jax import lax
from jax.experimental import pallas as pl
from jax.experimental.pallas import tpu as pltpu
from jax.sharding import PartitionSpec as P

MESH = pl.DeviceIdType.MESH
F32, BF = jnp.float32, jnp.bfloat16
VMEM, DMA, ds = pltpu.VMEM, pltpu.SemaphoreType.DMA, pl.ds
LN_EPS = 1e-5
HALF_SQRT, INV_SQRT_2PI = 0.7071067811865476, 0.3989422804014327
LOW, HIGH, NO_LABEL = -3e38, 3e38, -1e6
W, L, TILE = 1024, 128, 8
SEQS, SEQ, MASKS, SLOT = 6, 512, 77, 80
USED, TOK = SEQS * SLOT, 512
VROWS, ROWS, BLK = 3824, 3840, 384
N_BLK = ROWS // BLK
LAST = VROWS - (N_BLK - 1) * BLK
NCH = W // L
HALF, SH, SUB = ROWS // 2, ROWS // 8, ROWS // 32
CUT, SCUT = SH // 2, 64
SCUTS = (SCUT, SUB - SCUT)
QROWS, XROWS, XCUT = 128, 136, 72
VEC0, SMALL0, MINI = W, W + 24, 1280
MSH, MSUB = MINI // 8, MINI // 32
LOSS_ROW, N_SMALL = ROWS // L, 32
OTH0 = NCH * ROWS
DW0 = 2 * OTH0
MG0 = DW0 + 8 * W
TAIL0 = MG0 + MINI
OUT_ROWS = TAIL0 + MINI - W
NSTAGE = 8
NEAR, FAR = (1, 3), 2
AROUND = NEAR + (FAR,)
TWO, THREE = (0, 1), (0, 1, 2)


def sl(start, n):
    return ds(pl.multiple_of(start, TILE), n)


def wait_all(cps):
    for cp in cps:
        cp.wait()


def start_all(cps):
    for cp in cps:
        cp.start()


def gelu_norm(a):
    cdf = 0.5 * (1.0 + lax.erf(a * HALF_SQRT))
    g = a * cdf
    cen = g - jnp.mean(g, axis=-1, keepdims=True)
    rstd = lax.rsqrt(jnp.mean(cen * cen, axis=-1, keepdims=True) + LN_EPS)
    return cdf, rstd, cen * rstd


def dot(a, b, ca, cb):
    return lax.dot_general(a, b, (((ca,), (cb,)), ((), ())), preferred_element_type=F32)


def lanes(j):
    return ds(j * L, L)


def add_rows(dst, srcs, n, blk):
    def body(i, carry):
        r = sl(i * blk, blk)
        v = dst[r, :]
        for s in srcs:
            v = v + s[r, :]
        dst[r, :] = v
        return carry
    lax.fori_loop(0, n // blk, body, 0)


def head_kernel(scale, pos, lab_own, bias, vecs, hidden, emb, w_in, dz, aux, out,
                gt, u_all, r1, r2, r3, r4, a1, a2, part, drx, xr1, dabx, dwrx, m8, mr1, mr2,
                wbuf, zbuf, abuf, ztmp, lab_rx, stat, stats, small,
                ssem, rsem, psend, precv, sem_h, sem_w, es, er, st_s, st_r, xs, xr, ms, mr):
    dp, vp = lax.axis_index("dp"), lax.axis_index("vp")
    z, y, c = dp // 8, (dp // 2) % 4, dp % 2
    ynb = [z * 8 + ((y + d) % 4) * 2 + c for d in AROUND]
    znb = [((z + d) % 4) * 8 + y * 2 + c for d in AROUND]
    xnb = [(vp + d) % 4 for d in AROUND]
    mate = dp + 1 - 2 * c
    peers = [{"vp": v, "dp": d} for v in xnb for d in (dp, mate)] + [{"vp": vp, "dp": mate}]

    def load_hidden(b):
        r = sl(b * SEQ, SEQ)
        return pltpu.make_async_copy(hidden.at[r], gt.at[r], sem_h.at[b])

    def load_emb(i, slot, n):
        return pltpu.make_async_copy(emb.at[ds(pl.multiple_of(c * VROWS, 16) + i * BLK, n)],
                                     wbuf.at[ds(pl.multiple_of(slot * BLK, 16), n)], sem_w.at[slot])

    load_w = pltpu.make_async_copy(w_in, u_all, sem_h.at[SEQS])
    store_dz = pltpu.make_async_copy(u_all.at[ds(0, TOK)], dz, sem_h.at[0])
    load_w_again = pltpu.make_async_copy(w_in, gt.at[ds(0, W)], sem_h.at[SEQS])
    for b in range(SEQS):
        load_hidden(b).start()
    load_w.start()
    load_emb(0, 0, BLK).start()

    barrier = pltpu.get_barrier_semaphore()
    greet = peers + [{"dp": d} for d in ynb + znb]
    for d in greet:
        pl.semaphore_signal(barrier, inc=1, device_id=d, device_id_type=MESH)

    def remote(src, dst, send, recv, dev):
        return pltpu.make_async_remote_copy(src_ref=src, dst_ref=dst, send_sem=send, recv_sem=recv,
                                            device_id=dev, device_id_type=MESH)

    def to_mate(src, dst, i):
        return remote(src, dst, es.at[i], er.at[i], {"dp": mate})

    def to_x(src, dst, i, d):
        return remote(src, dst, xs.at[i, d], xr.at[i, d], {"vp": xnb[d]})

    c_u = [to_mate(part, drx, 0), to_mate(lab_own, lab_rx, 1)]
    own0 = pl.multiple_of(c * TOK, TOK)
    oth0 = pl.multiple_of((1 - c) * TOK, TOK)

    load_w.wait()

    def transform(b, carry):
        load_hidden(b).wait()
        where = jnp.broadcast_to(pos[ds(b, 1), :], (SEQ, L))
        hot = jnp.where(where == lax.broadcasted_iota(jnp.int32, (SEQ, L), 0), 1.0, 0.0).astype(BF)
        zrow = dot(hot, gt[sl(b * SEQ, SEQ), :], 0, 0)[:SLOT].astype(BF)
        ztmp[...] = zrow
        r = sl(b * SLOT, SLOT)
        zbuf[r, :] = ztmp[:, ds(pl.multiple_of(vp * 2 * L, L), 2 * L)]
        a = dot(zrow, u_all[...], 1, 0) + vecs[0:1, :]
        dabx[r, :] = a
        _, _, xhat = gelu_norm(a)
        part[r, :] = (xhat * vecs[1:2, :] + vecs[2:3, :]).astype(BF).astype(F32)
        return carry

    lax.fori_loop(0, SEQS, transform, 0)
    zbuf[ds(USED, TOK - USED), :] = jnp.zeros((TOK - USED, 2 * L), BF)
    part[ds(USED, TOK - USED), :] = jnp.zeros((TOK - USED, W), F32)
    dabx[ds(USED, TOK - USED), :] = jnp.zeros((TOK - USED, W), F32)
    abuf[...] = dabx[sl(vp * QROWS, QROWS), :]
    u_all[ds(own0, TOK), :] = part[...].astype(BF)
    pl.semaphore_wait(barrier, len(greet))
    start_all(c_u)

    def stream(body, init, again):
        def blk(i, carry):
            slot = i % 2
            for at, n in ((i + 2 < N_BLK, BLK), (i + 2 == N_BLK, LAST)):
                pl.when(at)(lambda: load_emb(i + 1, 1 - slot, n).start())
            if again:
                pl.when(i + 1 == N_BLK)(lambda: load_emb(0, 1 - slot, BLK).start())
            for at, n in ((i + 1 < N_BLK, BLK), (i + 1 == N_BLK, LAST)):
                pl.when(at)(lambda: load_emb(i, slot, n).wait())
            return body(i, wbuf[ds(pl.multiple_of(slot * BLK, 16), BLK), :], carry)
        return lax.fori_loop(0, N_BLK, blk, init)

    row0 = (vp * 2 * VROWS + c * VROWS).astype(F32)

    def local_labels(ref):
        v = ref[0:1, :] - row0
        return jnp.where((v >= 0) & (v < VROWS), v, -1.0)

    def logits(tok0, lab, again):
        u = u_all[ds(tok0, TOK), :]
        labs = jnp.broadcast_to(lab, (TILE, TOK)) - lax.broadcasted_iota(jnp.int32, (TILE, TOK), 0).astype(F32)

        def block(i, e, carry):
            mx, sm, lb = carry
            x = dot(e, u, 1, 1)
            col = [jnp.transpose(jnp.broadcast_to(bias[ds(c * LOSS_ROW + i * (BLK // L) + j, 1), :], (L, L)))
                   for j in range(BLK // L)]
            x = x + jnp.concatenate([jnp.concatenate(col, axis=0)] * (TOK // L), axis=1)
            for j in range(TOK // L):
                out[sl((tok0 // L + j) * ROWS + i * BLK, BLK), :] = x[:, j * L:(j + 1) * L]
            x = x.reshape(BLK // TILE, TILE, TOK)
            top = jnp.maximum(mx, jnp.max(x, axis=0))
            sm = sm * jnp.exp(mx - top) + jnp.sum(jnp.exp(x - top[None]), axis=0)
            ids = (lax.broadcasted_iota(jnp.int32, (BLK // TILE, TILE, TOK), 0) * TILE).astype(F32)
            lb = lb + jnp.sum(jnp.where(ids == (labs - (i * BLK).astype(F32))[None], x, 0.0), axis=0)
            return top, sm, lb

        zero = jnp.zeros((TILE, TOK), F32)
        mx, sm, lb = stream(block, (jnp.full((TILE, TOK), LOW, F32), zero, zero), again)
        top = jnp.max(mx, axis=0, keepdims=True)
        sm = jnp.sum(sm * jnp.exp(mx - top), axis=0, keepdims=True)
        lb = jnp.sum(lb, axis=0, keepdims=True)
        stat[:, ds(tok0, TOK)] = jnp.concatenate([top, sm, lb, jnp.zeros((TILE - 3, TOK), F32)], axis=0)

    lab1 = local_labels(lab_own)
    logits(own0, lab1, True)
    wait_all(c_u)
    u_all[ds(oth0, TOK), :] = drx[...].astype(BF)
    lab2 = local_labels(lab_rx)
    logits(oth0, lab2, True)
    c_st = [remote(stat, stats.at[j], st_s.at[j], st_r.at[j], d) for j, d in enumerate(peers)]
    start_all(c_st)
    wait_all(c_st)
    mx, sm, lb = (jnp.concatenate([stat[i:i + 1, :]] + [stats[j, i:i + 1, :] for j in range(len(peers))], axis=0)
                  for i in THREE)
    top = jnp.max(mx, axis=0, keepdims=True)
    norm = top + jnp.log(jnp.sum(sm * jnp.exp(mx - top), axis=0, keepdims=True))
    diff = norm - jnp.sum(lb, axis=0, keepdims=True)
    stat[0:1, :] = norm
    stat[1:2, :] = diff
    own_real = lab_own[0:1, :] >= 0
    diff = jnp.where(own_real, stat[1:2, ds(own0, TOK)], 0.0)
    small[ds(LOSS_ROW, 1), :] = sum(diff[:, j * L:(j + 1) * L] for j in range(TOK // L))
    small[ds(LOSS_ROW + 1, 1), :] = jnp.zeros((1, L), F32)
    for t0, ref, lab in ((own0, lab_own, lab1), (oth0, lab_rx, lab2)):
        stat[0:1, ds(t0, TOK)] = jnp.where(ref[0:1, :] >= 0, stat[0:1, ds(t0, TOK)], HIGH)
        stat[1:2, ds(t0, TOK)] = lab

    def grad(i, carry):
        ids = (lax.broadcasted_iota(jnp.int32, (L, L), 0) + i * L).astype(F32)
        s = jnp.zeros((L, L), F32)
        for j in range(2 * TOK // L):
            x = out[sl(j * ROWS + i * L, L), :]
            g = (jnp.exp(x - stat[0:1, lanes(j)]) - jnp.where(ids == stat[1:2, lanes(j)], 1.0, 0.0)) * scale
            gt[ds(pl.multiple_of(i * L, L), L), lanes(j)] = g.astype(BF)
            s = s + g
        small[ds(i, 1), :] = jnp.sum(jnp.transpose(s), axis=0, keepdims=True)
        return carry

    lax.fori_loop(0, ROWS // L, grad, 0)

    def rows(k, start, n):
        return out.at[sl(k * ROWS + start, n)]

    halves = []
    for b, p, pn, q, qn in ((0, y, ynb, z, znb), (HALF, z, znb, y, ynb)):
        pc, qc = ([(t + d) % 4 * n for d in NEAR] for t, n in ((p, SH), (q, SUB)))
        halves.append((b, pn, qn, pc, qc, b + (p + FAR) % 4 * SH, b + p * SH, (q + FAR) % 4 * SUB, q * SUB))

    def stage_copies(st, k):
        cps = []
        for h, (b, pn, qn, pc, qc, po, b2, qo, q0) in enumerate(halves):
            for d in TWO:
                n = SCUTS[d]
                if st == 0:
                    a = rows(k, po + d * CUT, CUT), r1.at[k % 2, h, d], pn
                elif st == 1:
                    a = rows(k, b + pc[d], SH), r2.at[k % 2, h, d], pn
                elif st == 2:
                    a = rows(k, b2 + qo + d * SCUT, n), r3.at[k % 2, h, d, ds(0, n)], qn
                elif st == 3:
                    a = rows(k, b2 + qc[d], SUB), r4.at[k % 2, h, d], qn
                elif st == 4:
                    a = rows(k, b2 + q0, SUB), a1.at[k % 3, h, d], qn
                elif st == 5:
                    a = a1.at[k % 3, h, d, ds(d * SCUT, n)], a2.at[k % 3, h, d, ds(0, n)], qn
                elif st == 6:
                    a = rows(k, b2, SH), rows(k, b2, SH), pn
                else:
                    s = rows(k, b + pc[1 - d] + d * CUT, CUT)
                    a = s, s, pn
                src, dst, nb = a
                cps.append(remote(src, dst, ssem.at[st, h, d, k], rsem.at[st, h, d, k], {"dp": nb[d]}))
        return cps

    def mate_copy(k):
        return remote(rows(k, 0, ROWS), rows(k, OTH0, ROWS), psend.at[k], precv.at[k], {"dp": mate})

    def stage(st, k):
        if st == 0:
            def mm(i, carry):
                rows(k, i * SH, SH)[...] = dot(gt[ds(pl.multiple_of(i * SH, 16), SH), :],
                                               u_all[:, ds(pl.multiple_of(k * L, L), L)], 1, 0)
                return carry
            lax.fori_loop(0, ROWS // SH, mm, 0)
        else:
            wait_all(stage_copies(st - 1, k))
            for h, (b, pn, qn, pc, qc, po, b2, qo, q0) in enumerate(halves):
                both = lambda r: [r.at[k % 2, h, d] for d in TWO]
                if st == 2:
                    add_rows(rows(k, b2, SH), both(r2), SH, SLOT)
                elif st == 4:
                    add_rows(rows(k, b2 + q0, SUB), both(r4), SUB, SUB)
                for d in TWO:
                    n = SCUTS[d]
                    if st == 1:
                        add_rows(rows(k, b + pc[d] + d * CUT, CUT), [r1.at[k % 2, h, d]], CUT, SLOT)
                    elif st == 3:
                        add_rows(rows(k, b2 + qc[d] + d * SCUT, n), [r3.at[k % 2, h, d]], n, n)
                    elif st == 5:
                        rows(k, b2 + qc[1 - d], SUB)[...] = a1[k % 3, h, d]
                    elif st == 6:
                        rows(k, b2 + qo + d * SCUT, n)[...] = a2[k % 3, h, d, ds(0, n)]
        if st < NSTAGE:
            start_all(stage_copies(st, k))
        else:
            mate_copy(k).start()

    xp, xm, xo = xnb

    def qrow(q, o, n):
        return sl(q * QROWS + o, n)

    def arow(q, o, n):
        return sl(q * XROWS + o, n)

    def same(ref, r):
        return ref.at[r], ref.at[r]

    def dwrow(j, o, n):
        return sl(DW0 + j * W + o, n)

    XTWO = ((xo, 0), (xo, QROWS // 2))
    c_du = [to_mate(part, drx, 2)]
    c_x1 = [to_x(drx.at[qrow(q, o, QROWS // 2)], xr1.at[d], 0, d) for d, (q, o) in enumerate(XTWO)]
    c_x2 = [to_x(drx.at[qrow(xnb[d], 0, QROWS)], part.at[ds(d * QROWS, QROWS)], 1, d) for d in TWO]
    c_x3 = [to_x(*same(dabx, arow(vp, 0, XROWS)), 2, d) for d in TWO]
    c_x4 = [to_x(*same(dabx, arow(q, o, n)), 3, d)
            for d, (q, o, n) in enumerate(((xm, 0, XCUT), (xp, XCUT, XROWS - XCUT)))]
    c_dw = [to_mate(part.at[qrow(1 - c, 0, QROWS)], dwrx.at[ds(0, QROWS)], 3),
            to_mate(part.at[ds(2 * QROWS, TILE)], dwrx.at[ds(QROWS, TILE)], 4)]
    c_w1 = [to_x(*same(out, dwrow(vp, 0, W)), 4, d) for d in TWO]
    c_w2 = [to_x(*same(out, dwrow(q, d * (W // 2), W // 2)), 5, d) for d, q in enumerate((xm, xp))]
    c_w3 = [to_mate(out.at[ds(DW0, 4 * W)], out.at[ds(DW0 + 4 * W, 4 * W)], 5),
            to_mate(out.at[ds(MG0 + W, MINI - W)], out.at[ds(TAIL0, MINI - W)], 6)]

    def du_part(col0, dst, again):
        def block(i, e, carry):
            dst[...] += dot(gt[ds(pl.multiple_of(i * BLK, L), BLK), ds(col0, TOK)], e, 0, 0)
            return carry
        stream(block, 0, again)

    def du_theirs():
        part[...] = jnp.zeros((TOK, W), F32)
        du_part(oth0, part, True)
        start_all(c_du)

    def du_mine():
        wait_all(c_du)
        du_part(own0, drx, False)

        def rnd(i, carry):
            r = sl(i * SCUT, SCUT)
            drx[r, :] = drx[r, :].astype(BF).astype(F32)
            return carry

        lax.fori_loop(0, TOK // SCUT, rnd, 0)
        start_all(c_x1)

    def du_near():
        wait_all(c_x1)
        for d, o in ((0, 0), (1, QROWS // 2)):
            drx[qrow(xnb[d], o, QROWS // 2), :] += xr1[d]
        start_all(c_x2)

    def norm_back():
        wait_all(c_x2)

        def block(i, sums):
            r = sl(i * 2 * TILE, 2 * TILE)
            a = abuf[r, :]
            dun = drx[qrow(vp, i * 2 * TILE, 2 * TILE), :] + part[r, :] + part[sl(QROWS + i * 2 * TILE, 2 * TILE), :]
            cdf, rstd, xhat = gelu_norm(a)
            dx = dun * vecs[1:2, :]
            dg = rstd * (dx - jnp.mean(dx, axis=-1, keepdims=True) - xhat * jnp.mean(dx * xhat, axis=-1, keepdims=True))
            da = dg * (cdf + a * jnp.exp(-0.5 * a * a) * INV_SQRT_2PI)
            dabx[arow(vp, i * 2 * TILE, 2 * TILE), :] = da.astype(BF).astype(F32)
            return tuple(s + t[:TILE] + t[TILE:] for s, t in zip(sums, (da, dun * xhat, dun)))

        sums = lax.fori_loop(0, QROWS // (2 * TILE), block, (jnp.zeros((TILE, W), F32),) * 3)
        sums = [jnp.sum(t, axis=0, keepdims=True) for t in sums]
        dabx[arow(vp, QROWS, TILE), :] = jnp.concatenate(sums + [jnp.zeros((TILE - 3, W), F32)], axis=0)
        start_all(c_x3)

    def pass_on():
        wait_all(c_x3)
        start_all(c_x4)

    def dab(q):
        return dabx[arow(q, 0, QROWS), :].astype(BF)

    def weight_grad():
        wait_all(c_x4)
        part[ds(0, 2 * QROWS), :] = sum(dot(zbuf[qrow(q, 0, QROWS), :], dab(q), 0, 0) for q in range(4))
        part[ds(2 * QROWS, TILE), :] = sum(dabx[arow(q, QROWS, TILE), :] for q in range(4))
        start_all(c_dw)

    def input_grad():
        load_w_again.start()
        wait_all(c_dw)
        for j in range(W // L):
            m8[lanes(j), :] = part[qrow(c, 0, QROWS), lanes(j)] + dwrx[ds(0, QROWS), lanes(j)]
            v = part[ds(2 * QROWS, TILE), lanes(j)] + dwrx[ds(QROWS, TILE), lanes(j)]
            for i in THREE:
                m8[ds(VEC0 + i * TILE + j, 1), :] = v[i:i + 1]
        m8[ds(SMALL0, N_SMALL), :] = small[...]
        m8[ds(SMALL0 + N_SMALL, MINI - SMALL0 - N_SMALL), :] = jnp.zeros((MINI - SMALL0 - N_SMALL, L), F32)
        start_all(mini_copies(0))

    mini = ((0, y, ynb, z, znb), (MINI // 2, z, znb, y, ynb))

    def mini_copies(st):
        cps = []
        for h, (b, p, pn, q, qn) in enumerate(mini):
            b2 = b + p * MSH
            for d, off in enumerate(AROUND):
                if st == 0:
                    a = m8.at[sl(b + (p + off) % 4 * MSH, MSH)], mr1.at[h, d], pn
                elif st == 1:
                    a = m8.at[sl(b2 + (q + off) % 4 * MSUB, MSUB)], mr2.at[h, d], qn
                elif st == 2:
                    a = *same(out, sl(MG0 + b2 + q * MSUB, MSUB)), qn
                else:
                    a = *same(out, sl(MG0 + b2, MSH)), pn
                src, dst, nb = a
                cps.append(remote(src, dst, ms.at[st, h, d], mr.at[st, h, d], {"dp": nb[d]}))
        return cps

    def mini_first():
        load_w_again.wait()
        for q in range(4):
            u_all[qrow(q, 0, QROWS), :] = dot(dab(q), gt[ds(0, W), :], 1, 1).astype(BF)
        store_dz.start()
        wait_all(mini_copies(0))
        for h, (b, p, pn, q, qn) in enumerate(mini):
            r = sl(b + p * MSH, MSH)
            m8[r, :] = m8[r, :] + sum(mr1[h, d] for d in THREE)
        start_all(mini_copies(1))

    def mini_second():
        store_dz.wait()
        wait_all(mini_copies(1))
        for h, (b, p, pn, q, qn) in enumerate(mini):
            r = b + p * MSH + q * MSUB
            out[sl(MG0 + r, MSUB), :] = m8[sl(r, MSUB), :] + sum(mr2[h, d] for d in THREE)
        start_all(mini_copies(2))

    def mini_third():
        wait_all(mini_copies(2))
        start_all(mini_copies(3))

    def weight_x():
        wait_all(mini_copies(3))
        out[dwrow(vp, 0, W), :] = out[ds(MG0, W), :]
        start_all(c_w1)

    def weight_on():
        wait_all(c_w1)
        start_all(c_w2)

    def weight_mate():
        wait_all(c_w2)
        start_all(c_w3)

    pieces = (du_theirs, du_mine, du_near, norm_back, pass_on, weight_grad, input_grad,
              mini_first, mini_second, mini_third, weight_x, weight_on, weight_mate)

    def step(t, carry):
        for st in reversed(range(NSTAGE + 1)):
            k = t - st
            pl.when((k >= 0) & (k < NCH))(functools.partial(stage, st, k))
        for at, piece in enumerate(pieces):
            pl.when(t == at + 1)(piece)
        return carry

    lax.fori_loop(0, NCH + NSTAGE, step, 0)

    def drain(k, carry):
        mate_copy(k).wait()
        return carry

    lax.fori_loop(0, NCH, drain, 0)
    wait_all(c_w3)
    save = [pltpu.make_async_copy(out.at[ds(r, MINI - W)], aux.at[j], sem_w.at[j]) for j, r in enumerate((MG0 + W, TAIL0))]
    start_all(save)
    wait_all(save)


def head_call(scale, pos, lab, bias, vecs, hidden, emb, w_in):
    vm, hbm = (pl.BlockSpec(memory_space=s) for s in (VMEM, pltpu.HBM))
    pair = (2, 2)
    sems = [(NSTAGE,) + pair + (NCH,)] * 2 + [(NCH,)] * 2 + [(SEQS + 1,), pair[:1]] + [(7,)] * 4 + [(6, 2)] * 2 + [(4, 2, 3)] * 2
    return pl.pallas_call(
        functools.partial(head_kernel, scale),
        out_shape=(jax.ShapeDtypeStruct((TOK, W), BF), jax.ShapeDtypeStruct((2, MINI - W, L), F32), VMEM((OUT_ROWS, L), F32)),
        in_specs=[vm] * 4 + [hbm] * 3,
        out_specs=(hbm, hbm, vm),
        scratch_shapes=[
            VMEM((ROWS, 2 * TOK), BF), VMEM((2 * TOK, W), BF),
            VMEM((2,) + pair + (CUT, L), F32), VMEM((2,) + pair + (SH, L), F32), VMEM((2,) + pair + (SCUT, L), F32),
            VMEM((2,) + pair + (SUB, L), F32), VMEM((3,) + pair + (SUB, L), F32), VMEM((3,) + pair + (SCUT, L), F32),
            VMEM((TOK, W), F32), VMEM((TOK, W), F32), VMEM((2, QROWS // 2, W), F32),
            VMEM((4 * XROWS, W), F32), VMEM((XROWS, W), F32), VMEM((MINI, L), F32), VMEM((2, 3, MSH, L), F32),
            VMEM((2, 3, MSUB, L), F32), VMEM((2 * BLK, W), BF), VMEM((TOK, 2 * L), BF), VMEM((QROWS, W), F32),
            VMEM((SLOT, W), BF), VMEM((TILE, TOK), F32), VMEM((TILE, 2 * TOK), F32), VMEM((7, TILE, 2 * TOK), F32),
            VMEM((N_SMALL, L), F32),
        ] + [DMA(s) for s in sems],
        compiler_params=pltpu.CompilerParams(collective_id=0, has_side_effects=True, vmem_limit_bytes=30560000),
        name="mlm_head",
    )(pos, lab, bias, vecs, hidden, emb, w_in)


def write_kernel(res, pos_in, dz_in, d_emb, d_w, d_hid, hid, pos, dz, sem, sem_w, sem_h, sem_i):
    c = lax.axis_index("dp") % 2
    cps = []
    for j, core in enumerate((c, 1 - c)):
        for k in range(NCH):
            cps.append(pltpu.make_async_copy(
                res.at[ds(j * OTH0 + k * ROWS, VROWS)], d_emb.at[sl(core * VROWS, VROWS), lanes(k)], sem.at[k, j]))
            for x in range(4):
                cps.append(pltpu.make_async_copy(
                    res.at[ds(DW0 + (j * 4 + x) * W + k * L, L)],
                    d_w.at[sl(x * 2 * L + core * L, L), lanes(k)], sem_w.at[k, j, x]))
    loads = [pltpu.make_async_copy(src, dst, sem_i.at[j]) for j, (src, dst) in enumerate(((pos_in, pos), (dz_in, dz)))]
    start_all(loads)
    start_all(cps)
    wait_all(loads)
    for b in range(SEQS):
        where = jnp.broadcast_to(pos[b:b + 1, :], (SEQ, L))
        hot = jnp.where(where == lax.broadcasted_iota(jnp.int32, (SEQ, L), 0), 1.0, 0.0).astype(BF)
        rows = jnp.concatenate([dz[b * SLOT:(b + 1) * SLOT, :], jnp.zeros((L - SLOT, W), BF)], axis=0)
        r = ds(b * SEQ, SEQ)
        hid[r, :] = dot(hot, rows, 1, 0).astype(BF)
        cp = pltpu.make_async_copy(hid.at[r], d_hid.at[r], sem_h.at[b])
        cp.start()
        cps.append(cp)
    wait_all(cps)


def write_call(res, pos, dz):
    vm, hbm = (pl.BlockSpec(memory_space=s) for s in (VMEM, pltpu.HBM))
    return pl.pallas_call(
        write_kernel,
        out_shape=tuple(jax.ShapeDtypeStruct(s, t) for s, t in (
            ((2 * VROWS, W), F32), ((W, W), F32), ((SEQS * SEQ, W), BF))),
        in_specs=[vm, hbm, hbm],
        out_specs=(hbm,) * 3,
        scratch_shapes=[VMEM((SEQS * SEQ, W), BF), VMEM((TILE, L), jnp.int32), VMEM((TOK, W), BF), DMA((NCH, 2)), DMA((NCH, 2, 4)),
                        DMA((SEQS,)), DMA((2,))],
        compiler_params=pltpu.CompilerParams(vmem_limit_bytes=16 << 20),
        name="write_rows",
    )(res, *(pltpu.with_memory_space_constraint(t, pltpu.HBM) for t in (pos, dz)))


def solution(mesh):
    n_groups = mesh.shape["dp"]

    def local_step(hidden, mask_pos, labels, w_trans, b_trans, ln_gain, ln_bias, emb_table, b_vocab):
        n_rows, seq_len, width = hidden.shape
        n_masks = mask_pos.shape[1]
        n_tokens = n_rows * n_masks * n_groups
        pos = jnp.pad(mask_pos, ((0, TILE - n_rows), (0, L - n_masks)), constant_values=-1)
        lab = jnp.pad(labels.astype(F32), ((0, 0), (0, SLOT - n_masks)), constant_values=NO_LABEL).reshape(1, USED)
        lab = jnp.broadcast_to(jnp.pad(lab, ((0, 0), (0, TOK - USED)), constant_values=NO_LABEL), (TILE, TOK))
        bias = jnp.pad(b_vocab.reshape(2, VROWS), ((0, 0), (0, ROWS - VROWS)), constant_values=LOW).reshape(2 * LOSS_ROW, L)
        vecs = jnp.stack([b_trans, ln_gain, ln_bias])
        dz, aux, res = head_call(1.0 / n_tokens, pos, lab, bias, vecs, hidden.reshape(n_rows * seq_len, width), emb_table, w_trans)
        d_emb, d_w_trans, d_hidden = write_call(res, pos, dz)
        aux, d_w_trans = lax.optimization_barrier((aux, d_w_trans))
        first = SMALL0 - VEC0
        vec = aux[0, :first].reshape(3, width)
        small = aux[:, first:first + N_SMALL]
        mlm_loss = jnp.sum(small[:, LOSS_ROW]) / n_tokens
        db = small.reshape(2, N_SMALL * L)[:, :VROWS]
        d_b_vocab = jnp.where(lax.axis_index("dp") % 2 == 0, db, db[::-1]).reshape(2 * VROWS)
        return (mlm_loss, d_hidden.reshape(hidden.shape), d_w_trans, vec[0], vec[1], vec[2], d_emb, d_b_vocab)

    in_specs = (P("dp", None, None), P("dp", None), P("dp", None), P(None, None), P(None), P(None), P(None), P("vp", None), P("vp"))
    out_specs = (P(), P("dp", None, None), P(None, None), P(None), P(None), P(None), P("vp", None), P("vp"))
    return jax.shard_map(local_step, mesh=mesh, in_specs=in_specs, out_specs=out_specs, check_vma=False)
```

time: 447 us -> 279 us (0.62)
  Pallas kernels: 0 us -> 265 us
  waiting for transfers between devices: 169 us -> 0 us
  blocking collectives: 135 us -> 0 us
  matrix products: 67.3 us -> 0 us
  other arithmetic: 28 us -> 3.35 us
  local copies, waits for them, and re-layouts: 30.5 us -> 7.03 us
  between operations: 16.1 us -> 2.49 us
    pallas_call x0 -> x2, Pallas kernels: none -> 265 us  [the longest x1 250 us: head_call(): pl.pallas_call(functools.partial(head_kernel, scale), out_shape=(jax.Shap...]
    psum x2 -> x0, waiting for transfers between devices: 169 us -> none  [the longest x1 129 us: local_step(): lax.psum(jnp.einsum('cle,clf->ef', masked_h, d_pre_bf, preferred_element_...]
    psum x1 -> x0, blocking collectives: 125 us -> none  [local_step(): mlm_loss = lax.psum(jnp.sum(log_norm - target), 'dp') / n_tokens]
    dot_general x7 -> x0, matrix products: 67.3 us -> none  [the longest x1 20.6 us: local_step(): jnp.einsum('cls,cle->se', d_logits_bf, u_bf16, preferred_element_type=jnp...]
    unnamed x32 -> x2, local copies, waits for them, and re-layouts: 29.9 us -> 0.79 us
    reduce_sum x10 -> x1, other arithmetic: 27.9 us -> 1.31 us  [local_step(): mlm_loss = jnp.sum(small[:, LOSS_ROW]) / n_tokens]
    all_gather x1 -> x0, blocking collectives: 10.3 us -> none  [local_step(): lax.all_gather(jnp.stack([local_max, local_sum, label_logit]), 'vp')]
  transfers between devices with their start and end apart: 2 -> 0, of which waited for: 2 -> 0; matrix products, arithmetic and copies ran while one was open for 8% -> 0% of each run, Pallas kernels for 0% -> 0%
where the time goes in v2:
time: 279 us; the launch traced here: 277 us
  Pallas kernels  265 us (95%)
  local copies, waits for them, and re-layouts  7.03 us (3%)
  other arithmetic  3.35 us (1%)
    pallas_call x1, Pallas kernels, head_call(): pl.pallas_call(functools.partial(head_kernel, scale), out_shape=(jax.Shap...  250 us
    pallas_call x1, Pallas kernels, write_call(): pl.pallas_call(write_kernel, out_shape=tuple((jax.ShapeDtypeStruct(s, t)...  14.1 us

profile of v2, /device:TPU:1, one launch (start us, length us, event | category | flops | bytes accessed | tf_op | source)
XLA Modules:
  0.0 277.4 jit_solution(18420928605591242214)
XLA Ops:
  0.6 1.3 pad.16.pos.pos_in
  1.9 0.7 convert_element_type.3
  2.6 0.1 reshape.43
  2.7 0.6 broadcast_in_dim.8.lab_own
  3.3 0.8 reshape.44
  4.2 0.6 reshape.45.bias
  4.8 1.3 pad_maximum_fusion.vecs
  6.2 250.4 %mlm_head.1 = (bf16[512,1024]{1,0:T(8,128)(2,1)}, f32[2,256,128]{2,1,0:T(8,128)}, f32[71168,128]{1,0:T(8,128)S(1)}) custom-call(s32[8,128]{1,0:T(8,128)} %pad.16.pos.pos_in, f32[8,512]{1,0:T(8,128)} %broadcast_in_dim.8.lab_own, f32[60,128]{1,0:T(8,128)} %reshape.45.bias, f32[3,1024]{1,0:T(4,128)} %pad_maximum_fusion.vecs, bf16[3072,1024]{1,0:T(8,128)(2,1)} %bitcast.17, ...), custom_call_target="tpu_custom_call" | custom-call | tf_op jit(solution)/shard_map/mlm_head/pallas_call | solution.py:486
  256.6 14.1 %write_rows.1 = (f32[7648,1024]{1,0:T(8,128)}, f32[1024,1024]{1,0:T(8,128)}, bf16[3072,1024]{1,0:T(8,128)(2,1)}) custom-call(f32[71168,128]{1,0:T(8,128)S(1)} %get-tuple-element.17.res, s32[8,128]{1,0:T(8,128)} %pad.16.pos.pos_in, bf16[512,1024]{1,0:T(8,128)(2,1)} %get-tuple-element.18.dz_in), custom_call_target="tpu_custom_call" | custom-call | tf_op jit(solution)/shard_map/write_rows/pallas_call | solution.py:535
  270.7 1.3 slice_reduce_fusion
  272.7 1.3 slice_bitcast_fusion.1
  274.0 0.8 slice_bitcast_fusion
  274.8 0.7 rev.3
  275.6 0.7 reshape.49
  (6 shorter events, 0.1 us)

commit v3 on v2

--- a/solution.py
+++ b/solution.py
@@ -79,9 +79,9 @@
     lax.fori_loop(0, n // blk, body, 0)
 
 
-def head_kernel(scale, pos, lab_own, bias, vecs, hidden, emb, w_in, dz, aux, out,
+def head_kernel(scale, pos_in, lab_in, b_in, b_trans, ln_gain, ln_bias, hidden, emb, w_in, dz, aux, out,
                 gt, u_all, r1, r2, r3, r4, a1, a2, part, drx, xr1, dabx, dwrx, m8, mr1, mr2,
-                wbuf, zbuf, abuf, ztmp, lab_rx, stat, stats, small,
+                wbuf, zbuf, abuf, pos, lab_own, bias, lab_rx, stat, stats, small,
                 ssem, rsem, psend, precv, sem_h, sem_w, es, er, st_s, st_r, xs, xr, ms, mr):
     dp, vp = lax.axis_index("dp"), lax.axis_index("vp")
     z, y, c = dp // 8, (dp // 2) % 4, dp % 2
@@ -126,26 +126,55 @@
     own0 = pl.multiple_of(c * TOK, TOK)
     oth0 = pl.multiple_of((1 - c) * TOK, TOK)
 
-    load_w.wait()
-
-    def transform(b, carry):
+    pos[...] = jnp.full((TILE, L), -1, jnp.int32)
+    pos[ds(0, SEQS), ds(0, MASKS)] = pos_in[...]
+    lane = lax.broadcasted_iota(jnp.int32, (L, TOK), 1)
+    seq = sum((lane >= b * SLOT).astype(jnp.int32) for b in range(1, SEQS))
+    slot = lane - seq * SLOT
+    place = jnp.where(slot == lax.broadcasted_iota(jnp.int32, (L, TOK), 0), 1.0, 0.0).astype(BF)[:MASKS]
+    high, low = lab_in[...] >> 8, lab_in[...] & 255
+    spread = dot(high.astype(F32).astype(BF), place, 1, 0) * 256.0 + dot(low.astype(F32).astype(BF), place, 1, 0)
+    row = lax.broadcasted_iota(jnp.int32, (SEQS, TOK), 0)
+    lab = jnp.sum(jnp.where(row == seq[:SEQS], spread, 0.0), axis=0, keepdims=True)
+    lab = jnp.where(slot[:1] < MASKS, lab, NO_LABEL)
+    lab_own[...] = jnp.broadcast_to(lab, (TILE, TOK))
+    rest = VROWS % L
+    for core in TWO:
+        @pl.when(c == core)
+        def _():
+            for i in range(VROWS // L):
+                bias[ds(i, 1), :] = b_in[:, core * VROWS + i * L:core * VROWS + (i + 1) * L]
+            bias[ds(LOSS_ROW - 1, 1), :] = jnp.full((1, L), LOW, F32)
+            bias[ds(LOSS_ROW - 1, 1), ds(0, rest)] = b_in[:, (core + 1) * VROWS - rest:(core + 1) * VROWS]
+
+    z0 = SEQS * SEQ
+
+    def gather(b, carry):
         load_hidden(b).wait()
         where = jnp.broadcast_to(pos[ds(b, 1), :], (SEQ, L))
         hot = jnp.where(where == lax.broadcasted_iota(jnp.int32, (SEQ, L), 0), 1.0, 0.0).astype(BF)
-        zrow = dot(hot, gt[sl(b * SEQ, SEQ), :], 0, 0)[:SLOT].astype(BF)
-        ztmp[...] = zrow
-        r = sl(b * SLOT, SLOT)
-        zbuf[r, :] = ztmp[:, ds(pl.multiple_of(vp * 2 * L, L), 2 * L)]
-        a = dot(zrow, u_all[...], 1, 0) + vecs[0:1, :]
-        dabx[r, :] = a
-        _, _, xhat = gelu_norm(a)
-        part[r, :] = (xhat * vecs[1:2, :] + vecs[2:3, :]).astype(BF).astype(F32)
+        gt[ds(pl.multiple_of(z0 + b * SLOT, 16), SLOT), :] = dot(hot, gt[sl(b * SEQ, SEQ), :], 0, 0)[:SLOT].astype(BF)
         return carry
 
-    lax.fori_loop(0, SEQS, transform, 0)
-    zbuf[ds(USED, TOK - USED), :] = jnp.zeros((TOK - USED, 2 * L), BF)
-    part[ds(USED, TOK - USED), :] = jnp.zeros((TOK - USED, W), F32)
-    dabx[ds(USED, TOK - USED), :] = jnp.zeros((TOK - USED, W), F32)
+    gt[ds(z0 + USED, TOK - USED), :] = jnp.zeros((TOK - USED, W), BF)
+    lax.fori_loop(0, SEQS, gather, 0)
+    load_w.wait()
+    zbuf[...] = gt[ds(z0, TOK), ds(pl.multiple_of(vp * 2 * L, L), 2 * L)]
+
+    def transform(i, carry):
+        r = sl(i * 2 * L, 2 * L)
+        dabx[r, :] = dot(gt[ds(pl.multiple_of(z0 + i * 2 * L, L), 2 * L), :], u_all[...], 1, 0) + b_trans[...]
+        return carry
+
+    lax.fori_loop(0, TOK // (2 * L), transform, 0)
+
+    def norm(i, carry):
+        r = sl(i * 4 * TILE, 4 * TILE)
+        _, _, xhat = gelu_norm(dabx[r, :])
+        part[r, :] = (xhat * ln_gain[...] + ln_bias[...]).astype(BF).astype(F32)
+        return carry
+
+    lax.fori_loop(0, TOK // (4 * TILE), norm, 0)
     abuf[...] = dabx[sl(vp * QROWS, QROWS), :]
     u_all[ds(own0, TOK), :] = part[...].astype(BF)
     pl.semaphore_wait(barrier, len(greet))
@@ -169,14 +198,13 @@
         v = ref[0:1, :] - row0
         return jnp.where((v >= 0) & (v < VROWS), v, -1.0)
 
-    def logits(tok0, lab, again):
+    def logits(tok0, again):
         u = u_all[ds(tok0, TOK), :]
-        labs = jnp.broadcast_to(lab, (TILE, TOK)) - lax.broadcasted_iota(jnp.int32, (TILE, TOK), 0).astype(F32)
 
         def block(i, e, carry):
-            mx, sm, lb = carry
+            mx, sm = carry
             x = dot(e, u, 1, 1)
-            col = [jnp.transpose(jnp.broadcast_to(bias[ds(c * LOSS_ROW + i * (BLK // L) + j, 1), :], (L, L)))
+            col = [jnp.transpose(jnp.broadcast_to(bias[ds(i * (BLK // L) + j, 1), :], (L, L)))
                    for j in range(BLK // L)]
             x = x + jnp.concatenate([jnp.concatenate(col, axis=0)] * (TOK // L), axis=1)
             for j in range(TOK // L):
@@ -184,53 +212,48 @@
             x = x.reshape(BLK // TILE, TILE, TOK)
             top = jnp.maximum(mx, jnp.max(x, axis=0))
             sm = sm * jnp.exp(mx - top) + jnp.sum(jnp.exp(x - top[None]), axis=0)
-            ids = (lax.broadcasted_iota(jnp.int32, (BLK // TILE, TILE, TOK), 0) * TILE).astype(F32)
-            lb = lb + jnp.sum(jnp.where(ids == (labs - (i * BLK).astype(F32))[None], x, 0.0), axis=0)
-            return top, sm, lb
-
-        zero = jnp.zeros((TILE, TOK), F32)
-        mx, sm, lb = stream(block, (jnp.full((TILE, TOK), LOW, F32), zero, zero), again)
+            return top, sm
+
+        mx, sm = stream(block, (jnp.full((TILE, TOK), LOW, F32), jnp.zeros((TILE, TOK), F32)), again)
         top = jnp.max(mx, axis=0, keepdims=True)
         sm = jnp.sum(sm * jnp.exp(mx - top), axis=0, keepdims=True)
-        lb = jnp.sum(lb, axis=0, keepdims=True)
-        stat[:, ds(tok0, TOK)] = jnp.concatenate([top, sm, lb, jnp.zeros((TILE - 3, TOK), F32)], axis=0)
+        stat[:, ds(tok0, TOK)] = jnp.concatenate([top, sm, jnp.zeros((TILE - 2, TOK), F32)], axis=0)
 
     lab1 = local_labels(lab_own)
-    logits(own0, lab1, True)
+    logits(own0, True)
     wait_all(c_u)
     u_all[ds(oth0, TOK), :] = drx[...].astype(BF)
     lab2 = local_labels(lab_rx)
-    logits(oth0, lab2, True)
+    logits(oth0, True)
     c_st = [remote(stat, stats.at[j], st_s.at[j], st_r.at[j], d) for j, d in enumerate(peers)]
     start_all(c_st)
     wait_all(c_st)
-    mx, sm, lb = (jnp.concatenate([stat[i:i + 1, :]] + [stats[j, i:i + 1, :] for j in range(len(peers))], axis=0)
-                  for i in THREE)
+    mx, sm = (jnp.concatenate([stat[i:i + 1, :]] + [stats[j, i:i + 1, :] for j in range(len(peers))], axis=0)
+              for i in TWO)
     top = jnp.max(mx, axis=0, keepdims=True)
     norm = top + jnp.log(jnp.sum(sm * jnp.exp(mx - top), axis=0, keepdims=True))
-    diff = norm - jnp.sum(lb, axis=0, keepdims=True)
     stat[0:1, :] = norm
-    stat[1:2, :] = diff
-    own_real = lab_own[0:1, :] >= 0
-    diff = jnp.where(own_real, stat[1:2, ds(own0, TOK)], 0.0)
-    small[ds(LOSS_ROW, 1), :] = sum(diff[:, j * L:(j + 1) * L] for j in range(TOK // L))
-    small[ds(LOSS_ROW + 1, 1), :] = jnp.zeros((1, L), F32)
+    own_norm = jnp.where(lab_own[0:1, :] >= 0, stat[0:1, ds(own0, TOK)], 0.0)
+    small[ds(LOSS_ROW, 1), :] = sum(own_norm[:, j * L:(j + 1) * L] for j in range(TOK // L))
     for t0, ref, lab in ((own0, lab_own, lab1), (oth0, lab_rx, lab2)):
         stat[0:1, ds(t0, TOK)] = jnp.where(ref[0:1, :] >= 0, stat[0:1, ds(t0, TOK)], HIGH)
         stat[1:2, ds(t0, TOK)] = lab
 
-    def grad(i, carry):
+    def grad(i, target):
         ids = (lax.broadcasted_iota(jnp.int32, (L, L), 0) + i * L).astype(F32)
         s = jnp.zeros((L, L), F32)
         for j in range(2 * TOK // L):
             x = out[sl(j * ROWS + i * L, L), :]
-            g = (jnp.exp(x - stat[0:1, lanes(j)]) - jnp.where(ids == stat[1:2, lanes(j)], 1.0, 0.0)) * scale
+            hit = ids == stat[1:2, lanes(j)]
+            g = (jnp.exp(x - stat[0:1, lanes(j)]) - jnp.where(hit, 1.0, 0.0)) * scale
             gt[ds(pl.multiple_of(i * L, L), L), lanes(j)] = g.astype(BF)
             s = s + g
+            target = target + jnp.where(hit, x, 0.0)
         small[ds(i, 1), :] = jnp.sum(jnp.transpose(s), axis=0, keepdims=True)
-        return carry
-
-    lax.fori_loop(0, ROWS // L, grad, 0)
+        return target
+
+    target = lax.fori_loop(0, ROWS // L, grad, jnp.zeros((L, L), F32))
+    small[ds(LOSS_ROW + 1, 1), :] = jnp.sum(target, axis=0, keepdims=True)
 
     def rows(k, start, n):
         return out.at[sl(k * ROWS + start, n)]
@@ -250,13 +273,13 @@
                 elif st == 1:
                     a = rows(k, b + pc[d], SH), r2.at[k % 2, h, d], pn
                 elif st == 2:
-                    a = rows(k, b2 + qo + d * SCUT, n), r3.at[k % 2, h, d, ds(0, n)], qn
+                    a = rows(k, b2 + qo + d * SCUT, n), r3.at[k % 3, h, d, ds(0, n)], qn
                 elif st == 3:
-                    a = rows(k, b2 + qc[d], SUB), r4.at[k % 2, h, d], qn
+                    a = rows(k, b2 + qc[d], SUB), r4.at[k % 3, h, d], qn
                 elif st == 4:
-                    a = rows(k, b2 + q0, SUB), a1.at[k % 3, h, d], qn
+                    a = rows(k, b2 + q0, SUB), a1.at[k % 4, h, d], qn
                 elif st == 5:
-                    a = a1.at[k % 3, h, d, ds(d * SCUT, n)], a2.at[k % 3, h, d, ds(0, n)], qn
+                    a = a1.at[k % 4, h, d, ds(d * SCUT, n)], a2.at[k % 3, h, d, ds(0, n)], qn
                 elif st == 6:
                     a = rows(k, b2, SH), rows(k, b2, SH), pn
                 else:
@@ -279,19 +302,19 @@
         else:
             wait_all(stage_copies(st - 1, k))
             for h, (b, pn, qn, pc, qc, po, b2, qo, q0) in enumerate(halves):
-                both = lambda r: [r.at[k % 2, h, d] for d in TWO]
+                both = lambda r, m: [r.at[k % m, h, d] for d in TWO]
                 if st == 2:
-                    add_rows(rows(k, b2, SH), both(r2), SH, SLOT)
+                    add_rows(rows(k, b2, SH), both(r2, 2), SH, SLOT)
                 elif st == 4:
-                    add_rows(rows(k, b2 + q0, SUB), both(r4), SUB, SUB)
+                    add_rows(rows(k, b2 + q0, SUB), both(r4, 3), SUB, SUB)
                 for d in TWO:
                     n = SCUTS[d]
                     if st == 1:
                         add_rows(rows(k, b + pc[d] + d * CUT, CUT), [r1.at[k % 2, h, d]], CUT, SLOT)
                     elif st == 3:
-                        add_rows(rows(k, b2 + qc[d] + d * SCUT, n), [r3.at[k % 2, h, d]], n, n)
+                        add_rows(rows(k, b2 + qc[d] + d * SCUT, n), [r3.at[k % 3, h, d]], n, n)
                     elif st == 5:
-                        rows(k, b2 + qc[1 - d], SUB)[...] = a1[k % 3, h, d]
+                        rows(k, b2 + qc[1 - d], SUB)[...] = a1[k % 4, h, d]
                     elif st == 6:
                         rows(k, b2 + qo + d * SCUT, n)[...] = a2[k % 3, h, d, ds(0, n)]
         if st < NSTAGE:
@@ -364,7 +387,7 @@
             a = abuf[r, :]
             dun = drx[qrow(vp, i * 2 * TILE, 2 * TILE), :] + part[r, :] + part[sl(QROWS + i * 2 * TILE, 2 * TILE), :]
             cdf, rstd, xhat = gelu_norm(a)
-            dx = dun * vecs[1:2, :]
+            dx = dun * ln_gain[...]
             dg = rstd * (dx - jnp.mean(dx, axis=-1, keepdims=True) - xhat * jnp.mean(dx * xhat, axis=-1, keepdims=True))
             da = dg * (cdf + a * jnp.exp(-0.5 * a * a) * INV_SQRT_2PI)
             dabx[arow(vp, i * 2 * TILE, 2 * TILE), :] = da.astype(BF).astype(F32)
@@ -372,7 +395,8 @@
 
         sums = lax.fori_loop(0, QROWS // (2 * TILE), block, (jnp.zeros((TILE, W), F32),) * 3)
         sums = [jnp.sum(t, axis=0, keepdims=True) for t in sums]
-        dabx[arow(vp, QROWS, TILE), :] = jnp.concatenate(sums + [jnp.zeros((TILE - 3, W), F32)], axis=0)
+        sums.append(jnp.concatenate([small[ds(LOSS_ROW + 1, 1), :], jnp.zeros((1, W - L), F32)], axis=1))
+        dabx[arow(vp, QROWS, TILE), :] = jnp.concatenate(sums + [jnp.zeros((TILE - len(sums), W), F32)], axis=0)
         start_all(c_x3)
 
     def pass_on():
@@ -396,6 +420,8 @@
             v = part[ds(2 * QROWS, TILE), lanes(j)] + dwrx[ds(QROWS, TILE), lanes(j)]
             for i in THREE:
                 m8[ds(VEC0 + i * TILE + j, 1), :] = v[i:i + 1]
+            if j == 0:
+                small[ds(LOSS_ROW + 1, 1), :] = v[3:4]
         m8[ds(SMALL0, N_SMALL), :] = small[...]
         m8[ds(SMALL0 + N_SMALL, MINI - SMALL0 - N_SMALL), :] = jnp.zeros((MINI - SMALL0 - N_SMALL, L), F32)
         start_all(mini_copies(0))
@@ -458,15 +484,19 @@
     pieces = (du_theirs, du_mine, du_near, norm_back, pass_on, weight_grad, input_grad,
               mini_first, mini_second, mini_third, weight_x, weight_on, weight_mate)
 
-    def step(t, carry):
-        for st in reversed(range(NSTAGE + 1)):
+    def step(stages, now, t, carry):
+        for st in stages:
             k = t - st
             pl.when((k >= 0) & (k < NCH))(functools.partial(stage, st, k))
-        for at, piece in enumerate(pieces):
-            pl.when(t == at + 1)(piece)
+        for at, piece in now:
+            pl.when(t == at)(piece)
         return carry
 
-    lax.fori_loop(0, NCH + NSTAGE, step, 0)
+    timed = list(enumerate(pieces, 1))
+    filling = functools.partial(step, range(NSTAGE - 1, -1, -1), [p for p in timed if p[0] < NCH])
+    emptying = functools.partial(step, range(1, NSTAGE + 1), [p for p in timed if p[0] >= NCH])
+    lax.fori_loop(0, NCH, filling, 0)
+    lax.fori_loop(NCH, NCH + NSTAGE, emptying, 0)
 
     def drain(k, carry):
         mate_copy(k).wait()
@@ -479,28 +509,28 @@
     wait_all(save)
 
 
-def head_call(scale, pos, lab, bias, vecs, hidden, emb, w_in):
+def head_call(scale, *args):
     vm, hbm = (pl.BlockSpec(memory_space=s) for s in (VMEM, pltpu.HBM))
     pair = (2, 2)
     sems = [(NSTAGE,) + pair + (NCH,)] * 2 + [(NCH,)] * 2 + [(SEQS + 1,), pair[:1]] + [(7,)] * 4 + [(6, 2)] * 2 + [(4, 2, 3)] * 2
     return pl.pallas_call(
         functools.partial(head_kernel, scale),
         out_shape=(jax.ShapeDtypeStruct((TOK, W), BF), jax.ShapeDtypeStruct((2, MINI - W, L), F32), VMEM((OUT_ROWS, L), F32)),
-        in_specs=[vm] * 4 + [hbm] * 3,
+        in_specs=[vm] * 6 + [hbm] * 3,
         out_specs=(hbm, hbm, vm),
         scratch_shapes=[
             VMEM((ROWS, 2 * TOK), BF), VMEM((2 * TOK, W), BF),
-            VMEM((2,) + pair + (CUT, L), F32), VMEM((2,) + pair + (SH, L), F32), VMEM((2,) + pair + (SCUT, L), F32),
-            VMEM((2,) + pair + (SUB, L), F32), VMEM((3,) + pair + (SUB, L), F32), VMEM((3,) + pair + (SCUT, L), F32),
+            VMEM((2,) + pair + (CUT, L), F32), VMEM((2,) + pair + (SH, L), F32), VMEM((3,) + pair + (SCUT, L), F32),
+            VMEM((3,) + pair + (SUB, L), F32), VMEM((4,) + pair + (SUB, L), F32), VMEM((3,) + pair + (SCUT, L), F32),
             VMEM((TOK, W), F32), VMEM((TOK, W), F32), VMEM((2, QROWS // 2, W), F32),
             VMEM((4 * XROWS, W), F32), VMEM((XROWS, W), F32), VMEM((MINI, L), F32), VMEM((2, 3, MSH, L), F32),
             VMEM((2, 3, MSUB, L), F32), VMEM((2 * BLK, W), BF), VMEM((TOK, 2 * L), BF), VMEM((QROWS, W), F32),
-            VMEM((SLOT, W), BF), VMEM((TILE, TOK), F32), VMEM((TILE, 2 * TOK), F32), VMEM((7, TILE, 2 * TOK), F32),
+            VMEM((TILE, L), jnp.int32), VMEM((TILE, TOK), F32), VMEM((N_SMALL, L), F32), VMEM((TILE, TOK), F32), VMEM((TILE, 2 * TOK), F32), VMEM((7, TILE, 2 * TOK), F32),
             VMEM((N_SMALL, L), F32),
         ] + [DMA(s) for s in sems],
         compiler_params=pltpu.CompilerParams(collective_id=0, has_side_effects=True, vmem_limit_bytes=30560000),
         name="mlm_head",
-    )(pos, lab, bias, vecs, hidden, emb, w_in)
+    )(*args)
 
 
 def write_kernel(res, pos_in, dz_in, d_emb, d_w, d_hid, hid, pos, dz, sem, sem_w, sem_h, sem_i):
@@ -519,7 +549,7 @@
     start_all(cps)
     wait_all(loads)
     for b in range(SEQS):
-        where = jnp.broadcast_to(pos[b:b + 1, :], (SEQ, L))
+        where = jnp.broadcast_to(jnp.concatenate([pos[b:b + 1, :], jnp.full((1, L - MASKS), -1, jnp.int32)], axis=1), (SEQ, L))
         hot = jnp.where(where == lax.broadcasted_iota(jnp.int32, (SEQ, L), 0), 1.0, 0.0).astype(BF)
         rows = jnp.concatenate([dz[b * SLOT:(b + 1) * SLOT, :], jnp.zeros((L - SLOT, W), BF)], axis=0)
         r = ds(b * SEQ, SEQ)
@@ -538,13 +568,40 @@
             ((2 * VROWS, W), F32), ((W, W), F32), ((SEQS * SEQ, W), BF))),
         in_specs=[vm, hbm, hbm],
         out_specs=(hbm,) * 3,
-        scratch_shapes=[VMEM((SEQS * SEQ, W), BF), VMEM((TILE, L), jnp.int32), VMEM((TOK, W), BF), DMA((NCH, 2)), DMA((NCH, 2, 4)),
+        scratch_shapes=[VMEM((SEQS * SEQ, W), BF), VMEM((SEQS, MASKS), jnp.int32), VMEM((TOK, W), BF), DMA((NCH, 2)), DMA((NCH, 2, 4)),
                         DMA((SEQS,)), DMA((2,))],
         compiler_params=pltpu.CompilerParams(vmem_limit_bytes=16 << 20),
         name="write_rows",
     )(res, *(pltpu.with_memory_space_constraint(t, pltpu.HBM) for t in (pos, dz)))
 
 
+def small_kernel(aux, b_trans, ln_gain, ln_bias, db, loss):
+    c = lax.axis_index("dp") % 2
+    for i, ref in enumerate((b_trans, ln_gain, ln_bias)):
+        ref[...] = aux[0, ds(i * TILE, TILE), :]
+    first, second = aux[ds(c, 1), ds(SMALL0 - VEC0, N_SMALL), :][0], aux[ds(1 - c, 1), ds(SMALL0 - VEC0, N_SMALL), :][0]
+    rest = VROWS % L
+    lane = lax.broadcasted_iota(jnp.int32, (LOSS_ROW, L), 1)
+    second = pltpu.roll(second, rest, 1)
+    db[ds(0, LOSS_ROW), :] = jnp.where((lane < rest) | (lax.broadcasted_iota(jnp.int32, (LOSS_ROW, L), 0) < LOSS_ROW - 1),
+                                       first[:LOSS_ROW], second[:1])
+    db[ds(LOSS_ROW, LOSS_ROW), :] = jnp.where(lane < rest, second[:LOSS_ROW], second[1:LOSS_ROW + 1])
+    at = SMALL0 - VEC0 + LOSS_ROW
+    total = aux[0, ds(at, 1), :] + aux[1, ds(at, 1), :] - aux[0, ds(at + 1, 1), :]
+    loss[...] = jnp.sum(total, axis=1, keepdims=True)
+
+
+def small_call(aux):
+    vm = pl.BlockSpec(memory_space=VMEM)
+    return pl.pallas_call(
+        small_kernel,
+        out_shape=tuple(jax.ShapeDtypeStruct(t, F32) for t in [(TILE, L)] * 3 + [(2 * LOSS_ROW, L), (1, 1)]),
+        in_specs=[vm],
+        out_specs=(vm,) * 5,
+        name="small_results",
+    )(aux)
+
+
 def solution(mesh):
     n_groups = mesh.shape["dp"]
 
@@ -552,21 +609,15 @@
         n_rows, seq_len, width = hidden.shape
         n_masks = mask_pos.shape[1]
         n_tokens = n_rows * n_masks * n_groups
-        pos = jnp.pad(mask_pos, ((0, TILE - n_rows), (0, L - n_masks)), constant_values=-1)
-        lab = jnp.pad(labels.astype(F32), ((0, 0), (0, SLOT - n_masks)), constant_values=NO_LABEL).reshape(1, USED)
-        lab = jnp.broadcast_to(jnp.pad(lab, ((0, 0), (0, TOK - USED)), constant_values=NO_LABEL), (TILE, TOK))
-        bias = jnp.pad(b_vocab.reshape(2, VROWS), ((0, 0), (0, ROWS - VROWS)), constant_values=LOW).reshape(2 * LOSS_ROW, L)
-        vecs = jnp.stack([b_trans, ln_gain, ln_bias])
-        dz, aux, res = head_call(1.0 / n_tokens, pos, lab, bias, vecs, hidden.reshape(n_rows * seq_len, width), emb_table, w_trans)
-        d_emb, d_w_trans, d_hidden = write_call(res, pos, dz)
+        line = lambda v: v.reshape(1, v.shape[0])
+        dz, aux, res = head_call(1.0 / n_tokens, mask_pos, labels, line(b_vocab), line(b_trans), line(ln_gain), line(ln_bias),
+                                 hidden.reshape(n_rows * seq_len, width), emb_table, w_trans)
+        d_emb, d_w_trans, d_hidden = write_call(res, mask_pos, dz)
         aux, d_w_trans = lax.optimization_barrier((aux, d_w_trans))
-        first = SMALL0 - VEC0
-        vec = aux[0, :first].reshape(3, width)
-        small = aux[:, first:first + N_SMALL]
-        mlm_loss = jnp.sum(small[:, LOSS_ROW]) / n_tokens
-        db = small.reshape(2, N_SMALL * L)[:, :VROWS]
-        d_b_vocab = jnp.where(lax.axis_index("dp") % 2 == 0, db, db[::-1]).reshape(2 * VROWS)
-        return (mlm_loss, d_hidden.reshape(hidden.shape), d_w_trans, vec[0], vec[1], vec[2], d_emb, d_b_vocab)
+        *vecs, db, loss = small_call(aux)
+        d_b_trans, d_gain, d_bias = (v.reshape(width) for v in vecs)
+        d_b_vocab = db.reshape(2 * ROWS)[:2 * VROWS]
+        return loss.reshape(()) / n_tokens, d_hidden.reshape(hidden.shape), d_w_trans, d_b_trans, d_gain, d_bias, d_emb, d_b_vocab
 
     in_specs = (P("dp", None, None), P("dp", None), P("dp", None), P(None, None), P(None), P(None), P(None), P("vp", None), P("vp"))
     out_specs = (P(), P("dp", None, None), P(None, None), P(None), P(None), P(None), P("vp", None), P("vp"))

time: 279 us -> 270 us (0.968)
  local copies, waits for them, and re-layouts: 7.03 us -> 1.39 us
  other arithmetic: 3.35 us -> 0 us
where the time goes in v3:
time: 270 us; the launch traced here: 269 us
  Pallas kernels  265 us (98%)
    pallas_call x1, Pallas kernels, head_call(): pl.pallas_call(functools.partial(head_kernel, scale), out_shape=(jax.Shap...  249 us
    pallas_call x1, Pallas kernels, write_call(): pl.pallas_call(write_kernel, out_shape=tuple((jax.ShapeDtypeStruct(s, t)...  14.1 us

profile of v3, /device:TPU:1, one launch (start us, length us, event | category | flops | bytes accessed | tf_op | source)
XLA Modules:
  0.0 268.9 jit_solution(13194510249791163426)
XLA Ops:
  0.6 1.4 reshape.49.b_in
  2.0 249.3 %mlm_head.1 = (bf16[512,1024]{1,0:T(8,128)(2,1)}, f32[2,256,128]{2,1,0:T(8,128)}, f32[71168,128]{1,0:T(8,128)S(1)}) custom-call(s32[6,77]{1,0:T(8,128)} %pos_in.3, s32[6,77]{1,0:T(8,128)} %lab_in.1, f32[1,7648]{1,0:T(1,128)} %reshape.49.b_in, f32[1,1024]{1,0:T(1,128)} %bitcast.12, f32[1,1024]{1,0:T(1,128)} %bitcast.13, f32[1,1024]{1,0:T(1,128)} %bitcast.14, ...), custom_call_target="tpu_custom_call" | custom-call | tf_op jit(solution)/shard_map/mlm_head/pallas_call | solution.py:516
  251.3 14.1 %write_rows.1 = (f32[7648,1024]{1,0:T(8,128)}, f32[1024,1024]{1,0:T(8,128)}, bf16[3072,1024]{1,0:T(8,128)(2,1)}) custom-call(f32[71168,128]{1,0:T(8,128)S(1)} %get-tuple-element.22.res, s32[6,77]{1,0:T(8,128)} %pos_in.3, bf16[512,1024]{1,0:T(8,128)(2,1)} %get-tuple-element.23.dz_in), custom_call_target="tpu_custom_call" | custom-call | tf_op jit(solution)/shard_map/write_rows/pallas_call | solution.py:565
  265.5 1.7 small_results.1

commit v4 on v3

--- a/solution.py
+++ b/solution.py
@@ -13,7 +13,7 @@
 LN_EPS = 1e-5
 HALF_SQRT, INV_SQRT_2PI = 0.7071067811865476, 0.3989422804014327
 LOW, HIGH, NO_LABEL = -3e38, 3e38, -1e6
-W, L, TILE = 1024, 128, 8
+W, L, TILE, BTILE = 1024, 128, 8, 16
 SEQS, SEQ, MASKS, SLOT = 6, 512, 77, 80
 USED, TOK = SEQS * SLOT, 512
 VROWS, ROWS, BLK = 3824, 3840, 384
@@ -55,12 +55,20 @@
 def gelu_norm(a):
     cdf = 0.5 * (1.0 + lax.erf(a * HALF_SQRT))
     g = a * cdf
-    cen = g - jnp.mean(g, axis=-1, keepdims=True)
-    rstd = lax.rsqrt(jnp.mean(cen * cen, axis=-1, keepdims=True) + LN_EPS)
+    cen = g - row_mean(g)
+    rstd = lax.rsqrt(row_mean(cen * cen) + LN_EPS)
     return cdf, rstd, cen * rstd
 
 
-def dot(a, b, ca, cb):
+def row_mean(t):
+    return jnp.mean(t, axis=-1, keepdims=True)
+
+
+def over_rows(fn, t):
+    return fn(t, axis=0, keepdims=True)
+
+
+def dot(a, b, ca=1, cb=0):
     return lax.dot_general(a, b, (((ca,), (cb,)), ((), ())), preferred_element_type=F32)
 
 
@@ -96,8 +104,8 @@
         return pltpu.make_async_copy(hidden.at[r], gt.at[r], sem_h.at[b])
 
     def load_emb(i, slot, n):
-        return pltpu.make_async_copy(emb.at[ds(pl.multiple_of(c * VROWS, 16) + i * BLK, n)],
-                                     wbuf.at[ds(pl.multiple_of(slot * BLK, 16), n)], sem_w.at[slot])
+        return pltpu.make_async_copy(emb.at[ds(pl.multiple_of(c * VROWS, BTILE) + i * BLK, n)],
+                                     wbuf.at[ds(pl.multiple_of(slot * BLK, BTILE), n)], sem_w.at[slot])
 
     load_w = pltpu.make_async_copy(w_in, u_all, sem_h.at[SEQS])
     store_dz = pltpu.make_async_copy(u_all.at[ds(0, TOK)], dz, sem_h.at[0])
@@ -133,9 +141,9 @@
     slot = lane - seq * SLOT
     place = jnp.where(slot == lax.broadcasted_iota(jnp.int32, (L, TOK), 0), 1.0, 0.0).astype(BF)[:MASKS]
     high, low = lab_in[...] >> 8, lab_in[...] & 255
-    spread = dot(high.astype(F32).astype(BF), place, 1, 0) * 256.0 + dot(low.astype(F32).astype(BF), place, 1, 0)
+    spread = dot(high.astype(F32).astype(BF), place) * 256.0 + dot(low.astype(F32).astype(BF), place)
     row = lax.broadcasted_iota(jnp.int32, (SEQS, TOK), 0)
-    lab = jnp.sum(jnp.where(row == seq[:SEQS], spread, 0.0), axis=0, keepdims=True)
+    lab = over_rows(jnp.sum, jnp.where(row == seq[:SEQS], spread, 0.0))
     lab = jnp.where(slot[:1] < MASKS, lab, NO_LABEL)
     lab_own[...] = jnp.broadcast_to(lab, (TILE, TOK))
     rest = VROWS % L
@@ -153,7 +161,7 @@
         load_hidden(b).wait()
         where = jnp.broadcast_to(pos[ds(b, 1), :], (SEQ, L))
         hot = jnp.where(where == lax.broadcasted_iota(jnp.int32, (SEQ, L), 0), 1.0, 0.0).astype(BF)
-        gt[ds(pl.multiple_of(z0 + b * SLOT, 16), SLOT), :] = dot(hot, gt[sl(b * SEQ, SEQ), :], 0, 0)[:SLOT].astype(BF)
+        gt[ds(pl.multiple_of(z0 + b * SLOT, BTILE), SLOT), :] = dot(hot, gt[sl(b * SEQ, SEQ), :], 0, 0)[:SLOT].astype(BF)
         return carry
 
     gt[ds(z0 + USED, TOK - USED), :] = jnp.zeros((TOK - USED, W), BF)
@@ -163,7 +171,7 @@
 
     def transform(i, carry):
         r = sl(i * 2 * L, 2 * L)
-        dabx[r, :] = dot(gt[ds(pl.multiple_of(z0 + i * 2 * L, L), 2 * L), :], u_all[...], 1, 0) + b_trans[...]
+        dabx[r, :] = dot(gt[ds(pl.multiple_of(z0 + i * 2 * L, L), 2 * L), :], u_all[...]) + b_trans[...]
         return carry
 
     lax.fori_loop(0, TOK // (2 * L), transform, 0)
@@ -181,16 +189,20 @@
     start_all(c_u)
 
     def stream(body, init, again):
-        def blk(i, carry):
-            slot = i % 2
-            for at, n in ((i + 2 < N_BLK, BLK), (i + 2 == N_BLK, LAST)):
-                pl.when(at)(lambda: load_emb(i + 1, 1 - slot, n).start())
+        def pair(m, carry):
+            last = m + 1 == N_BLK // 2
+            i = 2 * m
+            for at, n in ((~last, BLK), (last, LAST)):
+                pl.when(at)(load_emb(i + 1, 1, n).start)
+            load_emb(i, 0, BLK).wait()
+            carry = body(i, 0, wbuf[ds(0, BLK), :], carry)
+            pl.when(~last)(load_emb(i + 2, 0, BLK).start)
             if again:
-                pl.when(i + 1 == N_BLK)(lambda: load_emb(0, 1 - slot, BLK).start())
-            for at, n in ((i + 1 < N_BLK, BLK), (i + 1 == N_BLK, LAST)):
-                pl.when(at)(lambda: load_emb(i, slot, n).wait())
-            return body(i, wbuf[ds(pl.multiple_of(slot * BLK, 16), BLK), :], carry)
-        return lax.fori_loop(0, N_BLK, blk, init)
+                pl.when(last)(load_emb(0, 0, BLK).start)
+            for at, n in ((~last, BLK), (last, LAST)):
+                pl.when(at)(load_emb(i + 1, 1, n).wait)
+            return body(i + 1, 1, wbuf[ds(BLK, BLK), :], carry)
+        return lax.fori_loop(0, N_BLK // 2, pair, init)
 
     row0 = (vp * 2 * VROWS + c * VROWS).astype(F32)
 
@@ -201,22 +213,32 @@
     def logits(tok0, again):
         u = u_all[ds(tok0, TOK), :]
 
-        def block(i, e, carry):
-            mx, sm = carry
+        def sums(slot, top):
+            return jnp.concatenate(
+                [jnp.sum(jnp.exp(r2[slot, j // 2, j % 2, ds(0, BLK), :].reshape(BLK // TILE, TILE, L)
+                                 - top[:, j * L:(j + 1) * L][None]), axis=0) for j in range(TOK // L)], axis=1)
+
+        def block(i, slot, e, carry):
+            old, mx, sm = carry
+            sm = sm * jnp.exp(old - mx) + sums(1 - slot, mx)
             x = dot(e, u, 1, 1)
-            col = [jnp.transpose(jnp.broadcast_to(bias[ds(i * (BLK // L) + j, 1), :], (L, L)))
-                   for j in range(BLK // L)]
-            x = x + jnp.concatenate([jnp.concatenate(col, axis=0)] * (TOK // L), axis=1)
+            col = [jnp.transpose(jnp.broadcast_to(bias[ds(i * (BLK // L) + j, 1), :], (L, L))) for j in range(BLK // L)]
+            col = jnp.concatenate(col, axis=0)
+            top = []
             for j in range(TOK // L):
-                out[sl((tok0 // L + j) * ROWS + i * BLK, BLK), :] = x[:, j * L:(j + 1) * L]
-            x = x.reshape(BLK // TILE, TILE, TOK)
-            top = jnp.maximum(mx, jnp.max(x, axis=0))
-            sm = sm * jnp.exp(mx - top) + jnp.sum(jnp.exp(x - top[None]), axis=0)
-            return top, sm
-
-        mx, sm = stream(block, (jnp.full((TILE, TOK), LOW, F32), jnp.zeros((TILE, TOK), F32)), again)
-        top = jnp.max(mx, axis=0, keepdims=True)
-        sm = jnp.sum(sm * jnp.exp(mx - top), axis=0, keepdims=True)
+                v = x[:, j * L:(j + 1) * L] + col
+                out[sl((tok0 // L + j) * ROWS + i * BLK, BLK), :] = v
+                r2[slot, j // 2, j % 2, ds(0, BLK), :] = v
+                top.append(jnp.max(v.reshape(BLK // TILE, TILE, L), axis=0))
+            return mx, jnp.maximum(mx, jnp.concatenate(top, axis=1)), sm
+
+        low = jnp.full((TILE, TOK), LOW, F32)
+        for j in range(TOK // L):
+            r2[1, j // 2, j % 2, ds(0, BLK), :] = jnp.full((BLK, L), LOW, F32)
+        old, mx, sm = stream(block, (low, low, jnp.zeros((TILE, TOK), F32)), again)
+        sm = sm * jnp.exp(old - mx) + sums(1, mx)
+        top = over_rows(jnp.max, mx)
+        sm = over_rows(jnp.sum, sm * jnp.exp(mx - top))
         stat[:, ds(tok0, TOK)] = jnp.concatenate([top, sm, jnp.zeros((TILE - 2, TOK), F32)], axis=0)
 
     lab1 = local_labels(lab_own)
@@ -230,8 +252,8 @@
     wait_all(c_st)
     mx, sm = (jnp.concatenate([stat[i:i + 1, :]] + [stats[j, i:i + 1, :] for j in range(len(peers))], axis=0)
               for i in TWO)
-    top = jnp.max(mx, axis=0, keepdims=True)
-    norm = top + jnp.log(jnp.sum(sm * jnp.exp(mx - top), axis=0, keepdims=True))
+    top = over_rows(jnp.max, mx)
+    norm = top + jnp.log(over_rows(jnp.sum, sm * jnp.exp(mx - top)))
     stat[0:1, :] = norm
     own_norm = jnp.where(lab_own[0:1, :] >= 0, stat[0:1, ds(own0, TOK)], 0.0)
     small[ds(LOSS_ROW, 1), :] = sum(own_norm[:, j * L:(j + 1) * L] for j in range(TOK // L))
@@ -249,11 +271,11 @@
             gt[ds(pl.multiple_of(i * L, L), L), lanes(j)] = g.astype(BF)
             s = s + g
             target = target + jnp.where(hit, x, 0.0)
-        small[ds(i, 1), :] = jnp.sum(jnp.transpose(s), axis=0, keepdims=True)
+        small[ds(i, 1), :] = over_rows(jnp.sum, jnp.transpose(s))
         return target
 
     target = lax.fori_loop(0, ROWS // L, grad, jnp.zeros((L, L), F32))
-    small[ds(LOSS_ROW + 1, 1), :] = jnp.sum(target, axis=0, keepdims=True)
+    small[ds(LOSS_ROW + 1, 1), :] = over_rows(jnp.sum, target)
 
     def rows(k, start, n):
         return out.at[sl(k * ROWS + start, n)]
@@ -294,11 +316,18 @@
 
     def stage(st, k):
         if st == 0:
-            def mm(i, carry):
-                rows(k, i * SH, SH)[...] = dot(gt[ds(pl.multiple_of(i * SH, 16), SH), :],
-                                               u_all[:, ds(pl.multiple_of(k * L, L), L)], 1, 0)
+            def mm(r):
+                r = pl.multiple_of(r, BTILE)
+                rows(k, r, SH)[...] = dot(gt[ds(r, SH), :], u_all[:, ds(pl.multiple_of(k * L, L), L)])
+
+            for h in halves:
+                mm(h[5])
+            start_all(stage_copies(st, k))
+
+            def others(i, carry):
+                mm(i // 3 * HALF + (jnp.where(i < 3, y, z) + (i % 3 + 3)) % 4 * SH)
                 return carry
-            lax.fori_loop(0, ROWS // SH, mm, 0)
+            lax.fori_loop(0, 6, others, 0)
         else:
             wait_all(stage_copies(st - 1, k))
             for h, (b, pn, qn, pc, qc, po, b2, qo, q0) in enumerate(halves):
@@ -317,10 +346,10 @@
                         rows(k, b2 + qc[1 - d], SUB)[...] = a1[k % 4, h, d]
                     elif st == 6:
                         rows(k, b2 + qo + d * SCUT, n)[...] = a2[k % 3, h, d, ds(0, n)]
-        if st < NSTAGE:
+        if st == NSTAGE:
+            mate_copy(k).start()
+        elif st:
             start_all(stage_copies(st, k))
-        else:
-            mate_copy(k).start()
 
     xp, xm, xo = xnb
 
@@ -351,7 +380,7 @@
             to_mate(out.at[ds(MG0 + W, MINI - W)], out.at[ds(TAIL0, MINI - W)], 6)]
 
     def du_part(col0, dst, again):
-        def block(i, e, carry):
+        def block(i, slot, e, carry):
             dst[...] += dot(gt[ds(pl.multiple_of(i * BLK, L), BLK), ds(col0, TOK)], e, 0, 0)
             return carry
         stream(block, 0, again)
@@ -388,13 +417,13 @@
             dun = drx[qrow(vp, i * 2 * TILE, 2 * TILE), :] + part[r, :] + part[sl(QROWS + i * 2 * TILE, 2 * TILE), :]
             cdf, rstd, xhat = gelu_norm(a)
             dx = dun * ln_gain[...]
-            dg = rstd * (dx - jnp.mean(dx, axis=-1, keepdims=True) - xhat * jnp.mean(dx * xhat, axis=-1, keepdims=True))
+            dg = rstd * (dx - row_mean(dx) - xhat * row_mean(dx * xhat))
             da = dg * (cdf + a * jnp.exp(-0.5 * a * a) * INV_SQRT_2PI)
             dabx[arow(vp, i * 2 * TILE, 2 * TILE), :] = da.astype(BF).astype(F32)
             return tuple(s + t[:TILE] + t[TILE:] for s, t in zip(sums, (da, dun * xhat, dun)))
 
         sums = lax.fori_loop(0, QROWS // (2 * TILE), block, (jnp.zeros((TILE, W), F32),) * 3)
-        sums = [jnp.sum(t, axis=0, keepdims=True) for t in sums]
+        sums = [over_rows(jnp.sum, t) for t in sums]
         sums.append(jnp.concatenate([small[ds(LOSS_ROW + 1, 1), :], jnp.zeros((1, W - L), F32)], axis=1))
         dabx[arow(vp, QROWS, TILE), :] = jnp.concatenate(sums + [jnp.zeros((TILE - len(sums), W), F32)], axis=0)
         start_all(c_x3)
@@ -488,11 +517,16 @@
         for st in stages:
             k = t - st
             pl.when((k >= 0) & (k < NCH))(functools.partial(stage, st, k))
+            if st == NSTAGE // 2:
+                for at, piece in now:
+                    if piece is weight_grad:
+                        pl.when(t == at)(piece)
         for at, piece in now:
-            pl.when(t == at)(piece)
+            if piece is not weight_grad:
+                pl.when(t == at)(piece)
         return carry
 
-    timed = list(enumerate(pieces, 1))
+    timed = [(at, piece) for at, piece in zip((2, 3, 4, 5, 6, 7, 7, *range(NCH, NCH + 6)), pieces)]
     filling = functools.partial(step, range(NSTAGE - 1, -1, -1), [p for p in timed if p[0] < NCH])
     emptying = functools.partial(step, range(1, NSTAGE + 1), [p for p in timed if p[0] >= NCH])
     lax.fori_loop(0, NCH, filling, 0)
@@ -553,7 +587,7 @@
         hot = jnp.where(where == lax.broadcasted_iota(jnp.int32, (SEQ, L), 0), 1.0, 0.0).astype(BF)
         rows = jnp.concatenate([dz[b * SLOT:(b + 1) * SLOT, :], jnp.zeros((L - SLOT, W), BF)], axis=0)
         r = ds(b * SEQ, SEQ)
-        hid[r, :] = dot(hot, rows, 1, 0).astype(BF)
+        hid[r, :] = dot(hot, rows).astype(BF)
         cp = pltpu.make_async_copy(hid.at[r], d_hid.at[r], sem_h.at[b])
         cp.start()
         cps.append(cp)

time: 270 us -> 264 us (0.978)
  Pallas kernels: 265 us -> 259 us
    pallas_call x1, Pallas kernels: 249 us -> 243 us  [head_call(): pl.pallas_call(functools.partial(head_kernel, scale), out_shape=(jax.Shap...]
where the time goes in v4:
time: 264 us; the launch traced here: 263 us
  Pallas kernels  259 us (98%)
    pallas_call x1, Pallas kernels, head_call(): pl.pallas_call(functools.partial(head_kernel, scale), out_shape=(jax.Shap...  243 us
    pallas_call x1, Pallas kernels, write_call(): pl.pallas_call(write_kernel, out_shape=tuple((jax.ShapeDtypeStruct(s, t)...  14.1 us

profile of v4, /device:TPU:1, one launch (start us, length us, event | category | flops | bytes accessed | tf_op | source)
XLA Modules:
  0.0 262.7 jit_solution(9407646791482387953)
XLA Ops:
  0.6 1.4 reshape.49.b_in
  2.0 243.1 %mlm_head.1 = (bf16[512,1024]{1,0:T(8,128)(2,1)}, f32[2,256,128]{2,1,0:T(8,128)}, f32[71168,128]{1,0:T(8,128)S(1)}) custom-call(s32[6,77]{1,0:T(8,128)} %pos_in.3, s32[6,77]{1,0:T(8,128)} %lab_in.1, f32[1,7648]{1,0:T(1,128)} %reshape.49.b_in, f32[1,1024]{1,0:T(1,128)} %bitcast.12, f32[1,1024]{1,0:T(1,128)} %bitcast.13, f32[1,1024]{1,0:T(1,128)} %bitcast.14, ...), custom_call_target="tpu_custom_call" | custom-call | tf_op jit(solution)/shard_map/mlm_head/pallas_call | solution.py:550
  245.1 14.1 %write_rows.1 = (f32[7648,1024]{1,0:T(8,128)}, f32[1024,1024]{1,0:T(8,128)}, bf16[3072,1024]{1,0:T(8,128)(2,1)}) custom-call(f32[71168,128]{1,0:T(8,128)S(1)} %get-tuple-element.22.res, s32[6,77]{1,0:T(8,128)} %pos_in.3, bf16[512,1024]{1,0:T(8,128)(2,1)} %get-tuple-element.23.dz_in), custom_call_target="tpu_custom_call" | custom-call | tf_op jit(solution)/shard_map/write_rows/pallas_call | solution.py:599
  259.3 1.7 small_results.1

commit v5 on v4

--- a/solution.py
+++ b/solution.py
@@ -31,8 +31,9 @@
 DW0 = 2 * OTH0
 MG0 = DW0 + 8 * W
 TAIL0 = MG0 + MINI
-OUT_ROWS = TAIL0 + MINI - W
-NSTAGE = 8
+TAIL = 64
+OUT_ROWS = TAIL0 + TAIL
+NSTAGE, EARLY = 8, 3
 NEAR, FAR = (1, 3), 2
 AROUND = NEAR + (FAR,)
 TWO, THREE = (0, 1), (0, 1, 2)
@@ -291,7 +292,7 @@
             for d in TWO:
                 n = SCUTS[d]
                 if st == 0:
-                    a = rows(k, po + d * CUT, CUT), r1.at[k % 2, h, d], pn
+                    a = rows(k, po + d * CUT, CUT), r1.at[k % EARLY, h, d], pn
                 elif st == 1:
                     a = rows(k, b + pc[d], SH), r2.at[k % 2, h, d], pn
                 elif st == 2:
@@ -311,45 +312,55 @@
                 cps.append(remote(src, dst, ssem.at[st, h, d, k], rsem.at[st, h, d, k], {"dp": nb[d]}))
         return cps
 
-    def mate_copy(k):
-        return remote(rows(k, 0, ROWS), rows(k, OTH0, ROWS), psend.at[k], precv.at[k], {"dp": mate})
+    def mate_copies(k, far):
+        cps = []
+        for h, (b, pn, qn, pc, qc, po, b2, qo, q0) in enumerate(halves):
+            for i, r in enumerate([b2] + [b + t for t in pc] + [po]):
+                if far == (i == 3):
+                    cps.append(remote(rows(k, r, SH), rows(k, OTH0 + r, SH), psend.at[k, h, i], precv.at[k, h, i], {"dp": mate}))
+        return cps
+
+    def mm(k, r):
+        r = pl.multiple_of(r, BTILE)
+        rows(k, r, SH)[...] = dot(gt[ds(r, SH), :], u_all[:, ds(pl.multiple_of(k * L, L), L)])
+
+    def first_rows(k):
+        for h in halves:
+            mm(k, h[5])
+        start_all(stage_copies(0, k))
+
+    def other_rows(k):
+        def shard(i, carry):
+            mm(k, i // 3 * HALF + (jnp.where(i < 3, y, z) + (i % 3 + 3)) % 4 * SH)
+            return carry
+        lax.fori_loop(0, 6, shard, 0)
 
     def stage(st, k):
         if st == 0:
-            def mm(r):
-                r = pl.multiple_of(r, BTILE)
-                rows(k, r, SH)[...] = dot(gt[ds(r, SH), :], u_all[:, ds(pl.multiple_of(k * L, L), L)])
-
-            for h in halves:
-                mm(h[5])
+            first_rows(k)
+            other_rows(k)
+            return
+        wait_all(stage_copies(st - 1, k))
+        for h, (b, pn, qn, pc, qc, po, b2, qo, q0) in enumerate(halves):
+            both = lambda r, m: [r.at[k % m, h, d] for d in TWO]
+            if st == 2:
+                add_rows(rows(k, b2, SH), both(r2, 2), SH, SLOT)
+            elif st == 4:
+                add_rows(rows(k, b2 + q0, SUB), both(r4, 3), SUB, SUB)
+            for d in TWO:
+                n = SCUTS[d]
+                if st == 1:
+                    add_rows(rows(k, b + pc[d] + d * CUT, CUT), [r1.at[k % EARLY, h, d]], CUT, SLOT)
+                elif st == 3:
+                    add_rows(rows(k, b2 + qc[d] + d * SCUT, n), [r3.at[k % 3, h, d]], n, n)
+                elif st == 5:
+                    rows(k, b2 + qc[1 - d], SUB)[...] = a1[k % 4, h, d]
+                elif st == 6:
+                    rows(k, b2 + qo + d * SCUT, n)[...] = a2[k % 3, h, d, ds(0, n)]
+        if st < NSTAGE:
             start_all(stage_copies(st, k))
-
-            def others(i, carry):
-                mm(i // 3 * HALF + (jnp.where(i < 3, y, z) + (i % 3 + 3)) % 4 * SH)
-                return carry
-            lax.fori_loop(0, 6, others, 0)
-        else:
-            wait_all(stage_copies(st - 1, k))
-            for h, (b, pn, qn, pc, qc, po, b2, qo, q0) in enumerate(halves):
-                both = lambda r, m: [r.at[k % m, h, d] for d in TWO]
-                if st == 2:
-                    add_rows(rows(k, b2, SH), both(r2, 2), SH, SLOT)
-                elif st == 4:
-                    add_rows(rows(k, b2 + q0, SUB), both(r4, 3), SUB, SUB)
-                for d in TWO:
-                    n = SCUTS[d]
-                    if st == 1:
-                        add_rows(rows(k, b + pc[d] + d * CUT, CUT), [r1.at[k % 2, h, d]], CUT, SLOT)
-                    elif st == 3:
-                        add_rows(rows(k, b2 + qc[d] + d * SCUT, n), [r3.at[k % 3, h, d]], n, n)
-                    elif st == 5:
-                        rows(k, b2 + qc[1 - d], SUB)[...] = a1[k % 4, h, d]
-                    elif st == 6:
-                        rows(k, b2 + qo + d * SCUT, n)[...] = a2[k % 3, h, d, ds(0, n)]
-        if st == NSTAGE:
-            mate_copy(k).start()
-        elif st:
-            start_all(stage_copies(st, k))
+        if st + 1 >= NSTAGE:
+            start_all(mate_copies(k, st == NSTAGE))
 
     xp, xm, xo = xnb
 
@@ -377,7 +388,7 @@
     c_w1 = [to_x(*same(out, dwrow(vp, 0, W)), 4, d) for d in TWO]
     c_w2 = [to_x(*same(out, dwrow(q, d * (W // 2), W // 2)), 5, d) for d, q in enumerate((xm, xp))]
     c_w3 = [to_mate(out.at[ds(DW0, 4 * W)], out.at[ds(DW0 + 4 * W, 4 * W)], 5),
-            to_mate(out.at[ds(MG0 + W, MINI - W)], out.at[ds(TAIL0, MINI - W)], 6)]
+            to_mate(out.at[ds(MG0 + W, TAIL)], out.at[ds(TAIL0, TAIL)], 6)]
 
     def du_part(col0, dst, again):
         def block(i, slot, e, carry):
@@ -516,29 +527,29 @@
     def step(stages, now, t, carry):
         for st in stages:
             k = t - st
-            pl.when((k >= 0) & (k < NCH))(functools.partial(stage, st, k))
-            if st == NSTAGE // 2:
-                for at, piece in now:
-                    if piece is weight_grad:
-                        pl.when(t == at)(piece)
+            pl.when((k >= (0 if st else EARLY)) & (k < NCH))(functools.partial(stage, st, k))
         for at, piece in now:
-            if piece is not weight_grad:
-                pl.when(t == at)(piece)
+            pl.when(t == at)(piece)
         return carry
 
-    timed = [(at, piece) for at, piece in zip((2, 3, 4, 5, 6, 7, 7, *range(NCH, NCH + 6)), pieces)]
+    timed = [(at, piece) for at, piece in enumerate(pieces, 1)]
     filling = functools.partial(step, range(NSTAGE - 1, -1, -1), [p for p in timed if p[0] < NCH])
     emptying = functools.partial(step, range(1, NSTAGE + 1), [p for p in timed if p[0] >= NCH])
-    lax.fori_loop(0, NCH, filling, 0)
+    for k in range(EARLY):
+        first_rows(k)
+    for k in range(EARLY):
+        other_rows(k)
+    lax.fori_loop(1, NCH, filling, 0)
     lax.fori_loop(NCH, NCH + NSTAGE, emptying, 0)
 
     def drain(k, carry):
-        mate_copy(k).wait()
+        for far in (False, True):
+            wait_all(mate_copies(k, far))
         return carry
 
     lax.fori_loop(0, NCH, drain, 0)
     wait_all(c_w3)
-    save = [pltpu.make_async_copy(out.at[ds(r, MINI - W)], aux.at[j], sem_w.at[j]) for j, r in enumerate((MG0 + W, TAIL0))]
+    save = [pltpu.make_async_copy(out.at[ds(r, TAIL)], aux.at[j], sem_w.at[j]) for j, r in enumerate((MG0 + W, TAIL0))]
     start_all(save)
     wait_all(save)
 
@@ -546,15 +557,15 @@
 def head_call(scale, *args):
     vm, hbm = (pl.BlockSpec(memory_space=s) for s in (VMEM, pltpu.HBM))
     pair = (2, 2)
-    sems = [(NSTAGE,) + pair + (NCH,)] * 2 + [(NCH,)] * 2 + [(SEQS + 1,), pair[:1]] + [(7,)] * 4 + [(6, 2)] * 2 + [(4, 2, 3)] * 2
+    sems = [(NSTAGE,) + pair + (NCH,)] * 2 + [(NCH, 2, 4)] * 2 + [(SEQS + 1,), pair[:1]] + [(7,)] * 4 + [(6, 2)] * 2 + [(4, 2, 3)] * 2
     return pl.pallas_call(
         functools.partial(head_kernel, scale),
-        out_shape=(jax.ShapeDtypeStruct((TOK, W), BF), jax.ShapeDtypeStruct((2, MINI - W, L), F32), VMEM((OUT_ROWS, L), F32)),
+        out_shape=(jax.ShapeDtypeStruct((TOK, W), BF), jax.ShapeDtypeStruct((2, TAIL, L), F32), VMEM((OUT_ROWS, L), F32)),
         in_specs=[vm] * 6 + [hbm] * 3,
         out_specs=(hbm, hbm, vm),
         scratch_shapes=[
             VMEM((ROWS, 2 * TOK), BF), VMEM((2 * TOK, W), BF),
-            VMEM((2,) + pair + (CUT, L), F32), VMEM((2,) + pair + (SH, L), F32), VMEM((3,) + pair + (SCUT, L), F32),
+            VMEM((EARLY,) + pair + (CUT, L), F32), VMEM((2,) + pair + (SH, L), F32), VMEM((3,) + pair + (SCUT, L), F32),
             VMEM((3,) + pair + (SUB, L), F32), VMEM((4,) + pair + (SUB, L), F32), VMEM((3,) + pair + (SCUT, L), F32),
             VMEM((TOK, W), F32), VMEM((TOK, W), F32), VMEM((2, QROWS // 2, W), F32),
             VMEM((4 * XROWS, W), F32), VMEM((XROWS, W), F32), VMEM((MINI, L), F32), VMEM((2, 3, MSH, L), F32),
@@ -562,7 +573,7 @@
             VMEM((TILE, L), jnp.int32), VMEM((TILE, TOK), F32), VMEM((N_SMALL, L), F32), VMEM((TILE, TOK), F32), VMEM((TILE, 2 * TOK), F32), VMEM((7, TILE, 2 * TOK), F32),
             VMEM((N_SMALL, L), F32),
         ] + [DMA(s) for s in sems],
-        compiler_params=pltpu.CompilerParams(collective_id=0, has_side_effects=True, vmem_limit_bytes=30560000),
+        compiler_params=pltpu.CompilerParams(collective_id=0, has_side_effects=True, vmem_limit_bytes=30655000),
         name="mlm_head",
     )(*args)
 

time: 264 us -> 266 us (level)
  no operation moved by 1% of the time
where the time goes in v5:
time: 266 us; the launch traced here: 265 us
  Pallas kernels  261 us (98%)
    pallas_call x1, Pallas kernels, head_call(): pl.pallas_call(functools.partial(head_kernel, scale), out_shape=(jax.Shap...  245 us
    pallas_call x1, Pallas kernels, write_call(): pl.pallas_call(write_kernel, out_shape=tuple((jax.ShapeDtypeStruct(s, t)...  14.1 us

profile of v5, /device:TPU:1, one launch (start us, length us, event | category | flops | bytes accessed | tf_op | source)
XLA Modules:
  0.0 264.8 jit_solution(6236274660595992078)
XLA Ops:
  0.6 1.4 reshape.49.b_in
  2.0 245.3 %mlm_head.1 = (bf16[512,1024]{1,0:T(8,128)(2,1)}, f32[2,64,128]{2,1,0:T(8,128)}, f32[70976,128]{1,0:T(8,128)S(1)}) custom-call(s32[6,77]{1,0:T(8,128)} %pos_in.3, s32[6,77]{1,0:T(8,128)} %lab_in.1, f32[1,7648]{1,0:T(1,128)} %reshape.49.b_in, f32[1,1024]{1,0:T(1,128)} %bitcast.12, f32[1,1024]{1,0:T(1,128)} %bitcast.13, f32[1,1024]{1,0:T(1,128)} %bitcast.14, ...), custom_call_target="tpu_custom_call" | custom-call | tf_op jit(solution)/shard_map/mlm_head/pallas_call | solution.py:561
  247.3 14.1 %write_rows.1 = (f32[7648,1024]{1,0:T(8,128)}, f32[1024,1024]{1,0:T(8,128)}, bf16[3072,1024]{1,0:T(8,128)(2,1)}) custom-call(f32[70976,128]{1,0:T(8,128)S(1)} %get-tuple-element.22.res, s32[6,77]{1,0:T(8,128)} %pos_in.3, bf16[512,1024]{1,0:T(8,128)(2,1)} %get-tuple-element.23.dz_in), custom_call_target="tpu_custom_call" | custom-call | tf_op jit(solution)/shard_map/write_rows/pallas_call | solution.py:610
  261.5 1.5 small_results.1

commit v6 on v5

--- a/solution.py
+++ b/solution.py
@@ -1,4 +1,5 @@
 import functools
+import math
 
 import jax
 import jax.numpy as jnp
@@ -26,6 +27,7 @@
 QROWS, XROWS, XCUT = 128, 136, 72
 VEC0, SMALL0, MINI = W, W + 24, 1280
 MSH, MSUB = MINI // 8, MINI // 32
+MCUT = MSH // 2
 LOSS_ROW, N_SMALL = ROWS // L, 32
 OTH0 = NCH * ROWS
 DW0 = 2 * OTH0
@@ -37,6 +39,7 @@
 NEAR, FAR = (1, 3), 2
 AROUND = NEAR + (FAR,)
 TWO, THREE = (0, 1), (0, 1, 2)
+FIRST, SECOND = slice(0, 1), slice(1, 2)
 
 
 def sl(start, n):
@@ -208,7 +211,7 @@
     row0 = (vp * 2 * VROWS + c * VROWS).astype(F32)
 
     def local_labels(ref):
-        v = ref[0:1, :] - row0
+        v = ref[FIRST, :] - row0
         return jnp.where((v >= 0) & (v < VROWS), v, -1.0)
 
     def logits(tok0, again):
@@ -255,20 +258,20 @@
               for i in TWO)
     top = over_rows(jnp.max, mx)
     norm = top + jnp.log(over_rows(jnp.sum, sm * jnp.exp(mx - top)))
-    stat[0:1, :] = norm
-    own_norm = jnp.where(lab_own[0:1, :] >= 0, stat[0:1, ds(own0, TOK)], 0.0)
+    stat[FIRST, :] = norm
+    own_norm = jnp.where(lab_own[FIRST, :] >= 0, stat[FIRST, ds(own0, TOK)], 0.0)
     small[ds(LOSS_ROW, 1), :] = sum(own_norm[:, j * L:(j + 1) * L] for j in range(TOK // L))
     for t0, ref, lab in ((own0, lab_own, lab1), (oth0, lab_rx, lab2)):
-        stat[0:1, ds(t0, TOK)] = jnp.where(ref[0:1, :] >= 0, stat[0:1, ds(t0, TOK)], HIGH)
-        stat[1:2, ds(t0, TOK)] = lab
+        stat[FIRST, ds(t0, TOK)] = jnp.where(ref[FIRST, :] >= 0, stat[FIRST, ds(t0, TOK)] - math.log(scale), HIGH)
+        stat[SECOND, ds(t0, TOK)] = lab
 
     def grad(i, target):
         ids = (lax.broadcasted_iota(jnp.int32, (L, L), 0) + i * L).astype(F32)
         s = jnp.zeros((L, L), F32)
         for j in range(2 * TOK // L):
             x = out[sl(j * ROWS + i * L, L), :]
-            hit = ids == stat[1:2, lanes(j)]
-            g = (jnp.exp(x - stat[0:1, lanes(j)]) - jnp.where(hit, 1.0, 0.0)) * scale
+            hit = ids == stat[SECOND, lanes(j)]
+            g = jnp.exp(x - stat[FIRST, lanes(j)]) - jnp.where(hit, scale, 0.0)
             gt[ds(pl.multiple_of(i * L, L), L), lanes(j)] = g.astype(BF)
             s = s + g
             target = target + jnp.where(hit, x, 0.0)
@@ -472,44 +475,46 @@
         cps = []
         for h, (b, p, pn, q, qn) in enumerate(mini):
             b2 = b + p * MSH
-            for d, off in enumerate(AROUND):
+            direct = st in (2, 3)
+            for d, off in enumerate(AROUND if direct else NEAR):
+                half, near = d * MCUT, b + (p + off) % 4 * MSH
                 if st == 0:
-                    a = m8.at[sl(b + (p + off) % 4 * MSH, MSH)], mr1.at[h, d], pn
+                    a = m8.at[sl(b + (p + FAR) % 4 * MSH + half, MCUT)], mr1.at[h, FAR, ds(half, MCUT)]
                 elif st == 1:
-                    a = m8.at[sl(b2 + (q + off) % 4 * MSUB, MSUB)], mr2.at[h, d], qn
+                    a = m8.at[sl(near, MSH)], mr1.at[h, d]
                 elif st == 2:
-                    a = *same(out, sl(MG0 + b2 + q * MSUB, MSUB)), qn
+                    a = m8.at[sl(b2 + (q + off) % 4 * MSUB, MSUB)], mr2.at[h, d]
+                elif st == 3:
+                    a = same(out, sl(MG0 + b2 + q * MSUB, MSUB))
+                elif st == 4:
+                    a = same(out, sl(MG0 + b2, MSH))
                 else:
-                    a = *same(out, sl(MG0 + b2, MSH)), pn
-                src, dst, nb = a
-                cps.append(remote(src, dst, ms.at[st, h, d], mr.at[st, h, d], {"dp": nb[d]}))
+                    a = same(out, sl(MG0 + b + (p + NEAR[1 - d]) % 4 * MSH + half, MCUT))
+                cps.append(remote(*a, ms.at[st, h, d], mr.at[st, h, d], {"dp": (qn if direct else pn)[d]}))
         return cps
 
-    def mini_first():
+    def mini_step(st):
+        wait_all(mini_copies(st - 1))
+        for h, (b, p, pn, q, qn) in enumerate(mini):
+            if st == 1:
+                for d, off in enumerate(NEAR):
+                    m8[sl(b + (p + off) % 4 * MSH + d * MCUT, MCUT), :] += mr1[h, FAR, ds(d * MCUT, MCUT), :]
+            elif st == 2:
+                m8[sl(b + p * MSH, MSH), :] += mr1[h, 0] + mr1[h, 1]
+            elif st == 3:
+                r = b + p * MSH + q * MSUB
+                out[sl(MG0 + r, MSUB), :] = m8[sl(r, MSUB), :] + sum(mr2[h, d] for d in THREE)
+        start_all(mini_copies(st))
+
+    def hidden_grad():
         load_w_again.wait()
         for q in range(4):
             u_all[qrow(q, 0, QROWS), :] = dot(dab(q), gt[ds(0, W), :], 1, 1).astype(BF)
         store_dz.start()
-        wait_all(mini_copies(0))
-        for h, (b, p, pn, q, qn) in enumerate(mini):
-            r = sl(b + p * MSH, MSH)
-            m8[r, :] = m8[r, :] + sum(mr1[h, d] for d in THREE)
-        start_all(mini_copies(1))
-
-    def mini_second():
+
+    def weight_x():
         store_dz.wait()
-        wait_all(mini_copies(1))
-        for h, (b, p, pn, q, qn) in enumerate(mini):
-            r = b + p * MSH + q * MSUB
-            out[sl(MG0 + r, MSUB), :] = m8[sl(r, MSUB), :] + sum(mr2[h, d] for d in THREE)
-        start_all(mini_copies(2))
-
-    def mini_third():
-        wait_all(mini_copies(2))
-        start_all(mini_copies(3))
-
-    def weight_x():
-        wait_all(mini_copies(3))
+        wait_all(mini_copies(5))
         out[dwrow(vp, 0, W), :] = out[ds(MG0, W), :]
         start_all(c_w1)
 
@@ -521,20 +526,27 @@
         wait_all(c_w2)
         start_all(c_w3)
 
-    pieces = (du_theirs, du_mine, du_near, norm_back, pass_on, weight_grad, input_grad,
-              mini_first, mini_second, mini_third, weight_x, weight_on, weight_mate)
-
-    def step(stages, now, t, carry):
+    m = functools.partial
+    at_end = (du_theirs, du_mine, du_near, norm_back, pass_on, input_grad, hidden_grad, m(mini_step, 3), m(mini_step, 5),
+              weight_x, weight_on, weight_mate)
+    ends = list(enumerate(at_end, FAR))
+    middles = list(enumerate((weight_grad, m(mini_step, 1), m(mini_step, 2), m(mini_step, 4)), NCH - 1))
+
+    def step(stages, wanted, t, carry):
+        def run(pieces):
+            for at, piece in pieces:
+                if wanted(at):
+                    pl.when(t == at)(piece)
         for st in stages:
             k = t - st
-            pl.when((k >= (0 if st else EARLY)) & (k < NCH))(functools.partial(stage, st, k))
-        for at, piece in now:
-            pl.when(t == at)(piece)
+            pl.when((k >= (0 if st else EARLY)) & (k < NCH))(m(stage, st, k))
+            if st == NSTAGE // 2:
+                run(middles)
+        run(ends)
         return carry
 
-    timed = [(at, piece) for at, piece in enumerate(pieces, 1)]
-    filling = functools.partial(step, range(NSTAGE - 1, -1, -1), [p for p in timed if p[0] < NCH])
-    emptying = functools.partial(step, range(1, NSTAGE + 1), [p for p in timed if p[0] >= NCH])
+    filling = m(step, range(NSTAGE - 1, -1, -1), lambda at: at < NCH)
+    emptying = m(step, range(1, NSTAGE + 1), lambda at: at >= NCH)
     for k in range(EARLY):
         first_rows(k)
     for k in range(EARLY):
@@ -557,7 +569,7 @@
 def head_call(scale, *args):
     vm, hbm = (pl.BlockSpec(memory_space=s) for s in (VMEM, pltpu.HBM))
     pair = (2, 2)
-    sems = [(NSTAGE,) + pair + (NCH,)] * 2 + [(NCH, 2, 4)] * 2 + [(SEQS + 1,), pair[:1]] + [(7,)] * 4 + [(6, 2)] * 2 + [(4, 2, 3)] * 2
+    sems = [(NSTAGE,) + pair + (NCH,)] * 2 + [(NCH, 2, 4)] * 2 + [(SEQS + 1,), pair[:1]] + [(7,)] * 4 + [(6, 2)] * 2 + [(6, 2, 3)] * 2
     return pl.pallas_call(
         functools.partial(head_kernel, scale),
         out_shape=(jax.ShapeDtypeStruct((TOK, W), BF), jax.ShapeDtypeStruct((2, TAIL, L), F32), VMEM((OUT_ROWS, L), F32)),

time: 266 us -> 260 us (0.977)
  Pallas kernels: 261 us -> 255 us
    pallas_call x1, Pallas kernels: 245 us -> 239 us  [head_call(): pl.pallas_call(functools.partial(head_kernel, scale), out_shape=(jax.Shap...]
where the time goes in v6:
time: 260 us; the launch traced here: 259 us
  Pallas kernels  255 us (98%)
    pallas_call x1, Pallas kernels, head_call(): pl.pallas_call(functools.partial(head_kernel, scale), out_shape=(jax.Shap...  239 us
    pallas_call x1, Pallas kernels, write_call(): pl.pallas_call(write_kernel, out_shape=tuple((jax.ShapeDtypeStruct(s, t)...  14.1 us

profile of v6, /device:TPU:1, one launch (start us, length us, event | category | flops | bytes accessed | tf_op | source)
XLA Modules:
  0.0 258.9 jit_solution(5418708518738068939)
XLA Ops:
  0.6 1.4 reshape.49.b_in
  2.0 239.4 %mlm_head.1 = (bf16[512,1024]{1,0:T(8,128)(2,1)}, f32[2,64,128]{2,1,0:T(8,128)}, f32[70976,128]{1,0:T(8,128)S(1)}) custom-call(s32[6,77]{1,0:T(8,128)} %pos_in.3, s32[6,77]{1,0:T(8,128)} %lab_in.1, f32[1,7648]{1,0:T(1,128)} %reshape.49.b_in, f32[1,1024]{1,0:T(1,128)} %bitcast.12, f32[1,1024]{1,0:T(1,128)} %bitcast.13, f32[1,1024]{1,0:T(1,128)} %bitcast.14, ...), custom_call_target="tpu_custom_call" | custom-call | tf_op jit(solution)/shard_map/mlm_head/pallas_call | solution.py:573
  241.5 14.1 %write_rows.1 = (f32[7648,1024]{1,0:T(8,128)}, f32[1024,1024]{1,0:T(8,128)}, bf16[3072,1024]{1,0:T(8,128)(2,1)}) custom-call(f32[70976,128]{1,0:T(8,128)S(1)} %get-tuple-element.22.res, s32[6,77]{1,0:T(8,128)} %pos_in.3, bf16[512,1024]{1,0:T(8,128)(2,1)} %get-tuple-element.23.dz_in), custom_call_target="tpu_custom_call" | custom-call | tf_op jit(solution)/shard_map/write_rows/pallas_call | solution.py:622
  255.6 1.5 small_results.1

commit v7 on v6

--- a/solution.py
+++ b/solution.py
@@ -38,7 +38,8 @@
 NSTAGE, EARLY = 8, 3
 NEAR, FAR = (1, 3), 2
 AROUND = NEAR + (FAR,)
-TWO, THREE = (0, 1), (0, 1, 2)
+TWO, THREE, FOUR = (0, 1), (0, 1, 2), range(4)
+QW = TOK // 2
 FIRST, SECOND = slice(0, 1), slice(1, 2)
 
 
@@ -93,7 +94,7 @@
 
 def head_kernel(scale, pos_in, lab_in, b_in, b_trans, ln_gain, ln_bias, hidden, emb, w_in, dz, aux, out,
                 gt, u_all, r1, r2, r3, r4, a1, a2, part, drx, xr1, dabx, dwrx, m8, mr1, mr2,
-                wbuf, zbuf, abuf, pos, lab_own, bias, lab_rx, stat, stats, small,
+                wbuf, zbuf, abuf, pos, lab_own, bias, lab_rx, stat, msg, stats, small,
                 ssem, rsem, psend, precv, sem_h, sem_w, es, er, st_s, st_r, xs, xr, ms, mr):
     dp, vp = lax.axis_index("dp"), lax.axis_index("vp")
     z, y, c = dp // 8, (dp // 2) % 4, dp % 2
@@ -186,7 +187,8 @@
         part[r, :] = (xhat * ln_gain[...] + ln_bias[...]).astype(BF).astype(F32)
         return carry
 
-    lax.fori_loop(0, TOK // (4 * TILE), norm, 0)
+    lax.fori_loop(0, USED // (4 * TILE), norm, 0)
+    part[ds(USED, TOK - USED), :] = jnp.zeros((TOK - USED, W), F32)
     abuf[...] = dabx[sl(vp * QROWS, QROWS), :]
     u_all[ds(own0, TOK), :] = part[...].astype(BF)
     pl.semaphore_wait(barrier, len(greet))
@@ -251,14 +253,15 @@
     u_all[ds(oth0, TOK), :] = drx[...].astype(BF)
     lab2 = local_labels(lab_rx)
     logits(oth0, True)
-    c_st = [remote(stat, stats.at[j], st_s.at[j], st_r.at[j], d) for j, d in enumerate(peers)]
+    msg[...] = jnp.concatenate([stat[ds(i, 1), ds(j * QW, QW)] for i in TWO for j in FOUR], axis=0)
+    c_st = [remote(msg, stats.at[j], st_s.at[j], st_r.at[j], d) for j, d in enumerate(peers)]
     start_all(c_st)
     wait_all(c_st)
-    mx, sm = (jnp.concatenate([stat[i:i + 1, :]] + [stats[j, i:i + 1, :] for j in range(len(peers))], axis=0)
-              for i in TWO)
-    top = over_rows(jnp.max, mx)
-    norm = top + jnp.log(over_rows(jnp.sum, sm * jnp.exp(mx - top)))
-    stat[FIRST, :] = norm
+    for j in FOUR:
+        mx, sm = (jnp.concatenate([ref[ds(r, 1), :] for ref in (msg, *(stats.at[p] for p in range(len(peers))))], axis=0)
+                  for r in (j, j + len(FOUR)))
+        top = over_rows(jnp.max, mx)
+        stat[FIRST, ds(j * QW, QW)] = top + jnp.log(over_rows(jnp.sum, sm * jnp.exp(mx - top)))
     own_norm = jnp.where(lab_own[FIRST, :] >= 0, stat[FIRST, ds(own0, TOK)], 0.0)
     small[ds(LOSS_ROW, 1), :] = sum(own_norm[:, j * L:(j + 1) * L] for j in range(TOK // L))
     for t0, ref, lab in ((own0, lab_own, lab1), (oth0, lab_rx, lab2)):
@@ -451,8 +454,8 @@
 
     def weight_grad():
         wait_all(c_x4)
-        part[ds(0, 2 * QROWS), :] = sum(dot(zbuf[qrow(q, 0, QROWS), :], dab(q), 0, 0) for q in range(4))
-        part[ds(2 * QROWS, TILE), :] = sum(dabx[arow(q, QROWS, TILE), :] for q in range(4))
+        part[ds(0, 2 * QROWS), :] = sum(dot(zbuf[qrow(q, 0, QROWS), :], dab(q), 0, 0) for q in FOUR)
+        part[ds(2 * QROWS, TILE), :] = sum(dabx[arow(q, QROWS, TILE), :] for q in FOUR)
         start_all(c_dw)
 
     def input_grad():
@@ -508,7 +511,7 @@
 
     def hidden_grad():
         load_w_again.wait()
-        for q in range(4):
+        for q in FOUR:
             u_all[qrow(q, 0, QROWS), :] = dot(dab(q), gt[ds(0, W), :], 1, 1).astype(BF)
         store_dz.start()
 
@@ -582,7 +585,7 @@
             VMEM((TOK, W), F32), VMEM((TOK, W), F32), VMEM((2, QROWS // 2, W), F32),
             VMEM((4 * XROWS, W), F32), VMEM((XROWS, W), F32), VMEM((MINI, L), F32), VMEM((2, 3, MSH, L), F32),
             VMEM((2, 3, MSUB, L), F32), VMEM((2 * BLK, W), BF), VMEM((TOK, 2 * L), BF), VMEM((QROWS, W), F32),
-            VMEM((TILE, L), jnp.int32), VMEM((TILE, TOK), F32), VMEM((N_SMALL, L), F32), VMEM((TILE, TOK), F32), VMEM((TILE, 2 * TOK), F32), VMEM((7, TILE, 2 * TOK), F32),
+            VMEM((TILE, L), jnp.int32), VMEM((TILE, TOK), F32), VMEM((N_SMALL, L), F32), VMEM((TILE, TOK), F32), VMEM((TILE, 2 * TOK), F32), VMEM((TILE, QW), F32), VMEM((7, TILE, QW), F32),
             VMEM((N_SMALL, L), F32),
         ] + [DMA(s) for s in sems],
         compiler_params=pltpu.CompilerParams(collective_id=0, has_side_effects=True, vmem_limit_bytes=30655000),
@@ -597,7 +600,7 @@
         for k in range(NCH):
             cps.append(pltpu.make_async_copy(
                 res.at[ds(j * OTH0 + k * ROWS, VROWS)], d_emb.at[sl(core * VROWS, VROWS), lanes(k)], sem.at[k, j]))
-            for x in range(4):
+            for x in FOUR:
                 cps.append(pltpu.make_async_copy(
                     res.at[ds(DW0 + (j * 4 + x) * W + k * L, L)],
                     d_w.at[sl(x * 2 * L + core * L, L), lanes(k)], sem_w.at[k, j, x]))

time: 260 us -> 258 us (level)
  no operation moved by 1% of the time
where the time goes in v7:
time: 258 us; the launch traced here: 257 us
  Pallas kernels  253 us (98%)
    pallas_call x1, Pallas kernels, head_call(): pl.pallas_call(functools.partial(head_kernel, scale), out_shape=(jax.Shap...  238 us
    pallas_call x1, Pallas kernels, write_call(): pl.pallas_call(write_kernel, out_shape=tuple((jax.ShapeDtypeStruct(s, t)...  14.1 us

profile of v7, /device:TPU:1, one launch (start us, length us, event | category | flops | bytes accessed | tf_op | source)
XLA Modules:
  0.0 257.3 jit_solution(625800130924089089)
XLA Ops:
  0.6 1.4 reshape.49.b_in
  2.0 237.8 %mlm_head.1 = (bf16[512,1024]{1,0:T(8,128)(2,1)}, f32[2,64,128]{2,1,0:T(8,128)}, f32[70976,128]{1,0:T(8,128)S(1)}) custom-call(s32[6,77]{1,0:T(8,128)} %pos_in.3, s32[6,77]{1,0:T(8,128)} %lab_in.1, f32[1,7648]{1,0:T(1,128)} %reshape.49.b_in, f32[1,1024]{1,0:T(1,128)} %bitcast.12, f32[1,1024]{1,0:T(1,128)} %bitcast.13, f32[1,1024]{1,0:T(1,128)} %bitcast.14, ...), custom_call_target="tpu_custom_call" | custom-call | tf_op jit(solution)/shard_map/mlm_head/pallas_call | solution.py:576
  239.8 14.1 %write_rows.1 = (f32[7648,1024]{1,0:T(8,128)}, f32[1024,1024]{1,0:T(8,128)}, bf16[3072,1024]{1,0:T(8,128)(2,1)}) custom-call(f32[70976,128]{1,0:T(8,128)S(1)} %get-tuple-element.22.res, s32[6,77]{1,0:T(8,128)} %pos_in.3, bf16[512,1024]{1,0:T(8,128)(2,1)} %get-tuple-element.23.dz_in), custom_call_target="tpu_custom_call" | custom-call | tf_op jit(solution)/shard_map/write_rows/pallas_call | solution.py:625
  254.0 1.5 small_results.1
